TPU v7x, 32 devices: a whole 2x2x4 slice. The times are simulated.
32 devices in a mesh: gx: 4 (over x, core), gy: 2 (over y), gz: 4 (over z).
Axes of the slice: x: 2, y: 2, z: 4, core: 2. Of those that a mesh axis runs over, the one named last changes fastest.
Arguments:
- fields: float32 [5, 64, 16, 512], P(None, 'gz', 'gy', 'gx'), may hold values from -4 to 4
- radius: float32 [8, 64, 16, 512], P(None, 'gz', 'gy', 'gx'), may hold values from 0.4 to 1.5
- weight: float32 [8, 64, 16, 512], P(None, 'gz', 'gy', 'gx'), may hold values from 0.05 to 0.5
- column: int32 [8, 64, 16, 512], P(None, 'gz', 'gy', 'gx'), may hold values from 0 to 127
- counts: int32 [64, 16, 512], P('gz', 'gy', 'gx'), may hold values from 1 to 8
- fall_depth: int32 [8, 64, 16, 4], P(None, 'gz', 'gy', 'gx'), may hold values from 0 to 8, as said below
Outputs:
- new_fields: float32 [5, 64, 16, 512], P(None, 'gz', 'gy', 'gx')
- moments: float32 [3, 64, 16, 512], P(None, 'gz', 'gy', 'gx')
Inputs may be any that keep to these rules, and one draw needn't show every extreme that they name: The droplet in slot s of cell (k, j, i) sits in x cell (i // 128) * 128 + column[s, k, j, i]. Slots s < counts[k, j, i] hold live droplets. The droplets of slot s in cells (k, j, b * 128) to (k, j, (b + 1) * 128 - 1) fall together by fall_depth[s, k, j, b] levels, never below the lowest level: fall_depth[s, k, j, b] <= k; 8 is reached in every draw.
All inputs are finite; a program needn't handle non-finite values. Where the computation divides by a largest or mean magnitude, that divisor is 1e-20 or more.
Results may differ from a plain program's by a relative error of at most 0.00021.
Values sent between devices are 32-bit elements; how exact they have to be, the bound alone decides.
A program may use at most 64 MiB of HBM per device.

v0:
```python
import functools
import jax
import jax.numpy as jnp
from jax import lax
from jax.experimental import pallas as pl
from jax.experimental.pallas import tpu as pltpu
from jax.sharding import PartitionSpec as P

NS = 4
FMAX = 8
CELLS = 8
SLOT_LANES = 8

sound_speed = 10.0
buoyancy = 0.5
courant_goal = 0.6
growth = 0.3

MESH = pl.DeviceIdType.MESH
FULL = {0: 0, 1: 1, 3: 2}
THIN = {2: 0, 4: 1, 5: 2, 6: 3}
AXES = ("gy", "gx", "gz")


def flux(wind, a, b, c, d, e, f):
    central = 37.0 * (c + d) - 8.0 * (b + e) + (a + f)
    upwind = 10.0 * (d - c) - 5.0 * (e - b) + (f - a)
    return wind * central - jnp.abs(wind) * upwind


def kernel(
    sizes, depth_ref, fields_hbm, radius_hbm, weight_hbm, column_hbm, counts_hbm,
    out_fields, moments, *scratch
):
    names, levels, rows, cols, slots = sizes
    refs = dict(zip(names, scratch))
    radius, weight, column, counts = (refs[n] for n in ("radius", "weight", "column", "counts"))
    fields = refs["fields"]
    send_sem, recv_sem = refs["send_sem"], refs["recv_sem"]
    shape = (rows, cols)
    lane = lax.broadcasted_iota(jnp.int32, shape, 1)
    row = lax.broadcasted_iota(jnp.int32, shape, 0)
    place = {a: lax.axis_index(a) for a in AXES}
    count = {a: lax.axis_size(a) for a in AXES}
    has_low = place["gz"] > 0
    has_high = place["gz"] < count["gz"] - 1

    def lanes_by(x, shift):
        return pltpu.roll(x, shift % cols if isinstance(shift, int) else shift, 1)

    def rows_by(x, shift):
        return pltpu.roll(x, shift % rows, 0)

    def loop(n, body, carry, unroll=True):
        return lax.fori_loop(0, n, body, carry, unroll=unroll)

    fields_copy = pltpu.make_async_copy(fields_hbm, fields, refs["local_sem"].at[4])
    fields_copy.start()
    local = []
    for n, (src, dst) in enumerate(
        ((column_hbm, column), (counts_hbm, counts), (weight_hbm, weight), (radius_hbm, radius))
    ):
        copy = pltpu.make_async_copy(src, dst, refs["local_sem"].at[n])
        copy.start()
        local.append(copy)

    barrier = pltpu.get_barrier_semaphore()
    peers = 0
    for a in AXES:
        for step in range(1, count[a]):
            pl.semaphore_signal(
                barrier, inc=1,
                device_id={a: lax.rem(place[a] + step, count[a])}, device_id_type=MESH,
            )
            peers += 1

    fields_copy.wait()

    def first(k, top):
        w = fields[4, k]
        lid = jnp.where((k == levels - 1) & jnp.logical_not(has_high), 0.0, 1.0)
        w = w * lid
        refs["W0"][k + 1] = w
        refs["C0"][k + 3] = fields[0, k]
        refs["P0"][k + 3] = fields[1, k]
        refs["U0"][k] = fields[2, k]
        refs["V0"][k] = fields[3, k]
        return jnp.maximum(top, jnp.abs(fields[2, k]) + jnp.abs(fields[3, k]) + jnp.abs(w))

    top = loop(levels, first, jnp.zeros(shape, jnp.float32))
    pl.semaphore_wait(barrier, peers)

    def max_start(phase, value):
        a = AXES[phase]
        refs["max_send"][phase] = value
        copies = []
        for step in range(1, count[a]):
            copy = pltpu.make_async_remote_copy(
                src_ref=refs["max_send"].at[phase],
                dst_ref=refs["max_recv"].at[phase, step - 1],
                send_sem=refs["max_ss"].at[phase, step - 1],
                recv_sem=refs["max_rs"].at[phase, step - 1],
                device_id={a: lax.rem(place[a] + step, count[a])}, device_id_type=MESH,
            )
            copy.start()
            copies.append(copy)
        return copies

    def max_end(phase, value, copies):
        for n, copy in enumerate(copies):
            copy.wait()
            value = jnp.maximum(value, refs["max_recv"][phase, n])
        return value

    def neighbour(a, step):
        return {a: lax.rem(place[a] + count[a] + step, count[a])}

    def copies_of(e, wanted=("yu", "yd", "zu", "zd", "xu", "xd")):
        kind, at = ("f", FULL[e]) if e in FULL else ("t", THIN[e])
        out = {}
        for n, (name, a, step) in enumerate(
            (("yu", "gy", 1), ("yd", "gy", -1), ("zu", "gz", 1), ("zd", "gz", -1),
             ("xu", "gx", 1), ("xd", "gx", -1))
        ):
            if name not in wanted:
                continue
            out[name] = pltpu.make_async_remote_copy(
                src_ref=refs[kind + name + "_s"].at[at],
                dst_ref=refs[kind + name + "_r"].at[at],
                send_sem=send_sem.at[e, n],
                recv_sem=recv_sem.at[e, n],
                device_id=neighbour(a, step), device_id_type=MESH,
            )
        return out

    def send(e, tag):
        full = e in FULL
        kind, at = ("f", FULL[e]) if full else ("t", THIN[e])
        C, PR, U, V, W = (refs[n + tag] for n in "CPUVW")
        copies = copies_of(e)

        def pack_y(k, carry):
            p, v = PR[k + 3], V[k]
            if full:
                c = C[k + 3]
                refs["fyu_s"][at, k] = jnp.where(
                    row >= rows - 3, c, jnp.where(row == rows - 4, rows_by(v, -3), rows_by(p, -4))
                )
                refs["fyd_s"][at, k] = jnp.where(row < 3, c, rows_by(p, 3))
            else:
                refs["tyu_s"][at, pl.ds(k, 1), :] = p[rows - 1:rows]
                refs["tyu_s"][at, pl.ds(levels + k, 1), :] = v[rows - 1:rows]
                refs["tyd_s"][at, pl.ds(k, 1), :] = p[0:1]
            return carry

        loop(levels, pack_y, 0)
        width = 3 if full else 1
        for t in range(width):
            top_level = levels - width + t
            if full:
                refs["fzu_s"][at, t] = C[3 + top_level]
                refs["fzd_s"][at, t] = C[3 + t]
                refs["fzu_s"][at, 3 + t] = PR[3 + top_level]
                refs["fzd_s"][at, 3 + t] = PR[3 + t]
            else:
                refs["tzu_s"][at, 0] = PR[3 + top_level]
                refs["tzd_s"][at, 0] = PR[3]
        refs[kind + "zu_s"][at, 6 if full else 1] = W[levels]
        copies["yu"].start()
        copies["yd"].start()

        def pack_x(k, carry):
            up, down = carry
            p, u = PR[k + 3], U[k]
            if full:
                c = C[k + 3]
                high = jnp.where(
                    lane >= cols - 3, c,
                    jnp.where(lane == cols - 4, lanes_by(u, -3), lanes_by(p, -4)),
                )
                low = jnp.where(lane < 3, c, lanes_by(p, 3))
            else:
                high = jnp.where(lane == cols - 4, lanes_by(u, -3), lanes_by(p, -4))
                low = lanes_by(p, 3)
            here = lane // SLOT_LANES == k
            up = jnp.where(here, lanes_by(high, lax.rem(SLOT_LANES * (k + 1), cols)), up)
            down = jnp.where(here, lanes_by(low, SLOT_LANES * k), down)
            return up, down

        zero = jnp.zeros(shape, jnp.float32)
        up, down = loop(levels, pack_x, (zero, zero))
        refs[kind + "xu_s"][at] = up
        refs[kind + "xd_s"][at] = down

        @pl.when(has_high)
        def _():
            copies["zu"].start()

        @pl.when(has_low)
        def _():
            copies["zd"].start()

        copies["xu"].start()
        copies["xd"].start()

    def receive(e, tag):
        full = e in FULL
        kind, at = ("f", FULL[e]) if full else ("t", THIN[e])
        C, PR, W = (refs[n + tag] for n in "CPW")
        copies = copies_of(e, ("xu", "xd", "zu", "zd"))
        width = 3 if full else 1

        copies["xu"].wait()
        copies["xd"].wait()
        up, down = refs[kind + "xu_r"][at], refs[kind + "xd_r"][at]

        def unpack_x(k, carry):
            low = lanes_by(up, cols - SLOT_LANES * (k + 1))
            high = lanes_by(down, (cols - SLOT_LANES * k) % cols)
            if full:
                refs["HXC" + tag][k] = jnp.where(lane >= cols - 3, low, high)
            refs["HXP" + tag][k] = jnp.where(lane >= cols - 3, lanes_by(low, 4), lanes_by(high, -3))
            refs["HXU" + tag][k] = lanes_by(low, 3)
            return carry

        loop(levels, unpack_x, 0)

        @pl.when(has_high)
        def _():
            copies["zu"].wait_send()
            copies["zd"].wait_recv()
            for t in range(width):
                if full:
                    C[3 + levels + t] = refs["fzd_r"][at, t]
                    PR[3 + levels + t] = refs["fzd_r"][at, 3 + t]
                else:
                    PR[3 + levels + t] = refs["tzd_r"][at, t]

        @pl.when(jnp.logical_not(has_high))
        def _():
            for t in range(width):
                if full:
                    C[3 + levels + t] = jnp.zeros(shape, jnp.float32)
                PR[3 + levels + t] = jnp.zeros(shape, jnp.float32)

        @pl.when(has_low)
        def _():
            copies["zd"].wait_send()
            copies["zu"].wait_recv()
            for t in range(width):
                if full:
                    C[t] = refs["fzu_r"][at, t]
                    PR[t] = refs["fzu_r"][at, 3 + t]
                else:
                    PR[2] = refs["tzu_r"][at, 0]
            W[0] = refs[kind + "zu_r"][at, 6 if full else 1]

        @pl.when(jnp.logical_not(has_low))
        def _():
            for t in range(width):
                if full:
                    C[t] = jnp.zeros(shape, jnp.float32)
                PR[3 - width + t] = jnp.zeros(shape, jnp.float32)
            W[0] = jnp.zeros(shape, jnp.float32)

    def receive_y(e, tag):
        full = e in FULL
        at = FULL[e] if full else THIN[e]
        copies = copies_of(e, ("yu", "yd"))
        copies["yu"].wait()
        copies["yd"].wait()

        def unpack_y(k, carry):
            if full:
                low, high = refs["fyu_r"][at, k], refs["fyd_r"][at, k]
                refs["HYC" + tag][k] = jnp.where(row >= rows - 3, low, high)
                refs["HYP" + tag][k] = jnp.where(row >= rows - 3, rows_by(low, 4), rows_by(high, -3))
                refs["HYV" + tag][k] = rows_by(low, 3)
            else:
                low = refs["tyu_r"][at, pl.ds(k, 1), :]
                high = refs["tyd_r"][at, pl.ds(k, 1), :]
                refs["HYP" + tag][k] = jnp.where(row == rows - 1, low, high)
                refs["HYV" + tag][k] = jnp.broadcast_to(
                    refs["tyu_r"][at, pl.ds(levels + k, 1), :], shape
                )
            return carry

        loop(levels, unpack_y, 0)

    def sides(q, halo, by, index, extent):
        low = [by(jnp.where(index >= extent - n, halo, q), n) for n in (3, 2, 1)]
        high = [by(jnp.where(index < n, halo, q), -n) for n in (1, 2, 3)]
        return (*low, q, *high)

    def advect(tag, along_y):
        U, V, W = (refs[n + tag] for n in "UVW")

        def level(k, carry):
            u, w, w_low = U[k], W[k + 1], W[k]
            u_low = lanes_by(jnp.where(lane == cols - 1, refs["HXU" + tag][k], u), 1)
            for name, rate in (("C", "rate_c"), ("P", "rate_p")):
                Q = refs[name + tag]
                xs = sides(Q[k + 3], refs["HX" + name + tag][k], lanes_by, lane, cols)
                zs = [Q[k + n] for n in range(7)]
                total = flux(u, *xs[1:]) - flux(u_low, *xs[:6])
                refs[rate][k] = total + (flux(w, *zs[1:]) - flux(w_low, *zs[:6]))
            return carry

        def level_y(k, carry):
            v = V[k]
            v_low = rows_by(jnp.where(row == rows - 1, refs["HYV" + tag][k], v), 1)
            for name, rate in (("C", "rate_c"), ("P", "rate_p")):
                ys = sides(refs[name + tag][k + 3], refs["HY" + name + tag][k], rows_by, row, rows)
                total = refs[rate][k] + (flux(v, *ys[1:]) - flux(v_low, *ys[:6]))
                refs[rate][k] = total * (-1.0 / 60.0)
            return carry

        if along_y:
            loop(levels, level_y, 0, 8)
            return
        loop(levels, level, 0, 8)
        C = refs["C" + tag]
        lid_low = jnp.where(has_low, 1.0, 0.0)
        lid_high = jnp.where(has_high, 1.0, 0.0)
        for k in range(levels + 1):
            lift = (buoyancy * 0.5) * (C[k + 2] + C[k + 3])
            if k == 0:
                lift = lift * lid_low
            if k == levels:
                lift = lift * lid_high
            refs["lift"][k] = lift

    def substep(source, sub_step):
        SP, SU, SV, SW = (refs[n + source] for n in "PUVW")
        HXP, HXU, HYP, HYV = (refs[n + source] for n in ("HXP", "HXU", "HYP", "HYV"))
        DP, DU, DV, DW = (refs[n + "1"] for n in "PUVW")
        push = sub_step * sound_speed
        lid_low = jnp.where(has_low, 1.0, 0.0)

        def vertical(k):
            return SW[k] + sub_step * (
                refs["lift"][k] - sound_speed * (SP[k + 3] - SP[k + 2])
            )

        def level(k, w_low):
            p, u, v = SP[k + 3], SU[k], SV[k]
            hx, hy = HXP[k], HYP[k]
            lid = jnp.where((k == levels - 1) & jnp.logical_not(has_high), 0.0, 1.0)
            w = vertical(k + 1) * lid
            px = lanes_by(p, -1)
            py = rows_by(p, -1)
            u_new = u - push * (jnp.where(lane == cols - 1, lanes_by(hx, -1), px) - p)
            v_new = v - push * (jnp.where(row == rows - 1, rows_by(hy, -1), py) - p)
            u_halo = HXU[k] - push * (px - hx)
            v_halo = HYV[k] - push * (py - hy)
            u_low = lanes_by(jnp.where(lane == cols - 1, u_halo, u_new), 1)
            v_low = rows_by(jnp.where(row == rows - 1, v_halo, v_new), 1)
            div = (u_new - u_low) + (v_new - v_low) + (w - w_low)
            DU[k] = u_new
            DV[k] = v_new
            DW[k + 1] = w
            DP[k + 3] = p + sub_step * (refs["rate_p"][k] - sound_speed * div)
            return w

        loop(levels, level, vertical(0) * lid_low)

    def tracer(scale):
        def level(k, carry):
            refs["C1"][k + 3] = refs["C0"][k + 3] + scale * refs["rate_c"][k]
            return carry

        loop(levels, level, 0)

    acc, vals = refs["acc"], refs["vals"]

    def growth_terms():
        for n in range(4):
            local[n].wait()

        def cell(k, carry):
            c = refs["C1"][k + 3]
            live = counts[k]
            for s in range(slots):
                near = jnp.take_along_axis(c, column[s, k], axis=1, mode="promise_in_bounds")
                r = radius[s, k]
                squared = r * r * jnp.exp(growth * near)
                number = jnp.where(live > s, weight[s, k], 0.0)
                area = number * squared
                mass = area * jnp.sqrt(squared)
                for m, term in enumerate((number, area, mass)):
                    high = term.astype(jnp.bfloat16).astype(jnp.float32)
                    vals[s, k, m * rows:(m + 1) * rows, :] = high
                    vals[s, k, (m + 3) * rows:(m + 4) * rows, :] = term - high
                vals[s, k, 6 * rows:, :] = jnp.zeros((2 * rows, cols), jnp.float32)
            return carry

        loop(levels, cell, 0, 2)

    def clear():
        def level(k, carry):
            acc[k] = jnp.zeros((8 * rows, cols), jnp.float32)
            return carry

        loop(levels + FMAX, level, 0)

    def deposit(begin, end):
        ids = lax.broadcasted_iota(jnp.int32, (cols, cols), 0).astype(jnp.float32).astype(jnp.bfloat16)
        one = jnp.ones((cols, cols), jnp.bfloat16)
        none = jnp.zeros((cols, cols), jnp.bfloat16)
        zero = jnp.zeros((8, cols), jnp.float32)

        def cell(n, carry):
            k, j = begin + n // rows, n % rows
            by_depth = [None] * (FMAX + 1)
            for s in range(0, slots, 4):
                left, hots = [], []
                for t in range(4):
                    v = vals[s + t, k, pl.ds(j, 8, stride=rows), :]
                    left.append(jnp.concatenate([v, zero] if t % 2 == 0 else [zero, v], axis=1))
                    c = column[s + t, k, pl.ds(j, 1), :].astype(jnp.float32).astype(jnp.bfloat16)
                    hots.append(jnp.where(ids == jnp.broadcast_to(c, (cols, cols)), one, none))
                lhs = jnp.concatenate(left, axis=0).astype(jnp.bfloat16)
                rhs = jnp.concatenate(
                    [jnp.concatenate(hots[:2], axis=1), jnp.concatenate(hots[2:], axis=1)], axis=0
                )
                got = lax.dot_general(
                    lhs, rhs, (((1,), (1,)), ((), ())), preferred_element_type=jnp.float32
                )
                for t in range(4):
                    half = t // 2
                    part = got[8 * t:8 * (t + 1), half * cols:(half + 1) * cols]
                    depth = depth_ref[s + t, k * rows + j]
                    for d in range(FMAX + 1):
                        term = jnp.where(depth == d, part, 0.0)
                        by_depth[d] = term if by_depth[d] is None else by_depth[d] + term
            for d in range(FMAX + 1):
                at = pl.ds(pl.multiple_of(j * 8, 8), 8)
                acc[k + FMAX - d, at, :] = acc[k + FMAX - d, at, :] + by_depth[d]
            return carry

        lax.fori_loop(0, (end - begin) * rows, cell, 0, unroll=CELLS)

    def collect(m, l):
        return acc[l, pl.ds(m, rows, stride=8), :] + acc[l, pl.ds(m + 3, rows, stride=8), :]

    copies = max_start(0, top)
    send(0, "0")
    top = max_end(0, top, copies)
    copies = max_start(1, top)
    top = max_end(1, top, copies)
    copies = max_start(2, top)
    clear()
    receive(0, "0")
    advect("0", False)
    receive_y(0, "0")
    advect("0", True)
    top = max_end(2, top, copies)
    time_step = courant_goal / (1.0 + jnp.max(top, axis=(0, 1), keepdims=True))
    time_step = jnp.broadcast_to(time_step, shape)

    third = time_step * (1.0 / 3.0)
    tracer(third)
    substep("0", third)
    send(1, "1")
    receive(1, "1")
    advect("1", False)
    receive_y(1, "1")
    advect("1", True)
    half = time_step * 0.5
    tracer(half)
    part = half / (NS // 2)
    substep("0", part)
    send(2, "1")
    receive(2, "1")
    receive_y(2, "1")
    substep("1", part)
    send(3, "1")
    receive(3, "1")
    advect("1", False)
    receive_y(3, "1")
    advect("1", True)
    tracer(time_step)
    part = time_step / NS
    substep("0", part)
    send(4, "1")
    growth_terms()
    receive(4, "1")
    receive_y(4, "1")
    substep("1", part)
    send(5, "1")
    deposit(0, FMAX)
    moment_copy = pltpu.make_async_remote_copy(
        src_ref=refs["fall_s"], dst_ref=refs["fall_r"],
        send_sem=refs["fall_sem"].at[0], recv_sem=refs["fall_sem"].at[1],
        device_id=neighbour("gz", -1), device_id_type=MESH,
    )
    for m in range(3):
        for l in range(FMAX):
            refs["fall_s"][m, l] = collect(m, l)

    receive(5, "1")
    receive_y(5, "1")

    @pl.when(has_low)
    def _():
        moment_copy.start()

    substep("1", part)
    send(6, "1")
    deposit(FMAX, levels)
    receive(6, "1")
    receive_y(6, "1")
    substep("1", part)

    def write(k, carry):
        out_fields[0, k] = refs["C1"][k + 3]
        out_fields[1, k] = refs["P1"][k + 3]
        out_fields[2, k] = refs["U1"][k]
        out_fields[3, k] = refs["V1"][k]
        out_fields[4, k] = refs["W1"][k + 1]
        return carry

    loop(levels, write, 0)
    for m in range(3):
        for l in range(levels):
            moments[m, l] = collect(m, l + FMAX)

    @pl.when(has_low)
    def _():
        moment_copy.wait_send()

    @pl.when(has_high)
    def _():
        moment_copy.wait_recv()
        for m in range(3):
            for l in range(FMAX):
                at = levels - FMAX + l
                moments[m, at] = moments[m, at] + refs["fall_r"][m, l]


def per_device(fields, radius, weight, column, counts, fall_depth):
    levels, rows, cols = fields.shape[1:]
    slots = radius.shape[0]
    assert slots % 4 == 0 and levels * SLOT_LANES <= cols and rows == 8 and FMAX <= levels
    f32 = jnp.float32
    cell = (rows, cols)
    widest = max(lax.axis_size(a) for a in AXES) - 1
    spaces = {}

    def add(name, *shape, dtype=f32):
        spaces[name] = pltpu.VMEM(shape, dtype)

    add("fields", *fields.shape)
    add("radius", *radius.shape)
    add("weight", *weight.shape)
    add("column", *column.shape, dtype=jnp.int32)
    add("counts", *counts.shape, dtype=jnp.int32)
    for tag in "01":
        add("C" + tag, levels + 6, *cell)
        add("P" + tag, levels + 6, *cell)
        add("U" + tag, levels, *cell)
        add("V" + tag, levels, *cell)
        add("W" + tag, levels + 1, *cell)
        for name in ("HXC", "HXP", "HXU", "HYC", "HYP", "HYV"):
            add(name + tag, levels, *cell)
    add("rate_c", levels, *cell)
    add("rate_p", levels, *cell)
    add("lift", levels + 1, *cell)
    add("max_send", 3, *cell)
    add("max_recv", 3, widest, *cell)
    for end in ("_s", "_r"):
        for name, shape in (
            ("fxu", cell), ("fxd", cell), ("fyu", (levels,) + cell), ("fyd", (levels,) + cell),
            ("fzu", (7,) + cell), ("fzd", (6,) + cell),
        ):
            add(name + end, len(FULL), *shape)
        for name, shape in (
            ("txu", cell), ("txd", cell), ("tyu", (2 * levels, cols)), ("tyd", (levels, cols)),
            ("tzu", (2,) + cell), ("tzd", (1,) + cell),
        ):
            add(name + end, len(THIN), *shape)
    add("acc", levels + FMAX, 8 * rows, cols)
    add("vals", slots, levels, 8 * rows, cols)
    add("fall_s", 3, FMAX, *cell)
    add("fall_r", 3, FMAX, *cell)
    rounds = len(FULL) + len(THIN)
    spaces["send_sem"] = pltpu.SemaphoreType.DMA((rounds, 6))
    spaces["recv_sem"] = pltpu.SemaphoreType.DMA((rounds, 6))
    spaces["max_ss"] = pltpu.SemaphoreType.DMA((3, widest))
    spaces["max_rs"] = pltpu.SemaphoreType.DMA((3, widest))
    spaces["fall_sem"] = pltpu.SemaphoreType.DMA((2,))
    spaces["local_sem"] = pltpu.SemaphoreType.DMA((5,))
    vmem = pl.BlockSpec(memory_space=pltpu.VMEM)
    anywhere = pl.BlockSpec(memory_space=pltpu.HBM)
    return pl.pallas_call(
        functools.partial(kernel, (tuple(spaces), levels, rows, cols, slots)),
        out_shape=(
            jax.ShapeDtypeStruct(fields.shape, f32),
            jax.ShapeDtypeStruct((3, levels, rows, cols), f32),
        ),
        in_specs=[pl.BlockSpec(memory_space=pltpu.SMEM)] + [anywhere] * 5,
        out_specs=(vmem, vmem),
        scratch_shapes=list(spaces.values()),
        compiler_params=pltpu.CompilerParams(
            collective_id=0, has_side_effects=True, vmem_limit_bytes=48 * 1024 * 1024
        ),
        name="slab_step",
    )(fall_depth.reshape(slots, levels * rows), fields, radius, weight, column, counts)


def solution(mesh):
    in_specs = (
        P(None, "gz", "gy", "gx"),
        P(None, "gz", "gy", "gx"),
        P(None, "gz", "gy", "gx"),
        P(None, "gz", "gy", "gx"),
        P("gz", "gy", "gx"),
        P(None, "gz", "gy", "gx"),
    )
    out_specs = (P(None, "gz", "gy", "gx"), P(None, "gz", "gy", "gx"))
    return jax.shard_map(
        per_device, mesh=mesh, in_specs=in_specs, out_specs=out_specs, check_vma=False
    )
```

profile of v0, /device:TPU:0, one launch (start us, length us, event | category | flops | bytes accessed | tf_op | source)
XLA Modules:
  0.0 54.2 jit_solution(11721475607268897502)
XLA Ops:
  0.6 0.0 copy-start.4
  0.6 0.9 %copy.9 = s32[8,16,8,1]{2,1,0,3:T(8,128)S(1)} copy(s32[8,16,8,1]{1,3,2,0:T(1,128)} %param.11) | data formatting | bytes 8192 | tf_op args[5]
  1.5 0.1 reshape.7.depth_ref
  1.6 0.0 copy-done.4
  1.6 0.0 copy-start
  1.6 1.0 %copy-done = f32[8,16,8,128]{3,2,1,0:T(8,128)S(1)} copy-done((f32[8,16,8,128]{3,2,1,0:T(8,128)S(1)}, f32[8,16,8,128]{3,2,1,0:T(8,128)}, u32[]{:S(2)}) %copy-start) | copy-done | bytes 524312
  2.7 0.0 copy-start.1
  2.7 1.0 %copy-done.1 = f32[8,16,8,128]{3,2,1,0:T(8,128)S(1)} copy-done((f32[8,16,8,128]{3,2,1,0:T(8,128)S(1)}, f32[8,16,8,128]{3,2,1,0:T(8,128)}, u32[]{:S(2)}) %copy-start.1) | copy-done | bytes 524312
  3.7 0.0 copy-start.2
  3.7 1.0 %copy-done.2 = s32[8,16,8,128]{3,2,1,0:T(8,128)S(1)} copy-done((s32[8,16,8,128]{3,2,1,0:T(8,128)S(1)}, s32[8,16,8,128]{3,2,1,0:T(8,128)}, u32[]{:S(2)}) %copy-start.2) | copy-done | bytes 524312
  4.7 0.0 copy-start.3
  4.7 1.0 %copy-done.3 = f32[5,16,8,128]{3,2,1,0:T(8,128)S(1)} copy-done((f32[5,16,8,128]{3,2,1,0:T(8,128)S(1)}, f32[5,16,8,128]{3,2,1,0:T(8,128)}, u32[]{:S(2)}) %copy-start.3) | copy-done | bytes 327704
  5.7 47.1 %slab_step.1 = (f32[5,16,8,128]{3,2,1,0:T(8,128)S(1)}, f32[3,16,8,128]{3,2,1,0:T(8,128)S(1)}) custom-call(s32[8,128]{1,0:T(8,128)S(1)} %reshape.7.depth_ref, f32[5,16,8,128]{3,2,1,0:T(8,128)S(1)} %copy-done.3, f32[8,16,8,128]{3,2,1,0:T(8,128)S(1)} %copy-done, f32[8,16,8,128]{3,2,1,0:T(8,128)S(1)} %copy-done.1, s32[8,16,8,128]{3,2,1,0:T(8,128)S(1)} %copy-done.2, ...), custom_call_target="tpu_custom_call" | custom-call | tf_op jit(solution)/shard_map/slab_step/pallas_call | solution.py:595
  52.8 0.7 %copy.12 = f32[5,16,8,128]{3,2,1,0:T(8,128)} copy(f32[5,16,8,128]{3,2,1,0:T(8,128)S(1)} %get-tuple-element.4) | data formatting | bytes 655360
  53.6 0.7 %copy.13 = f32[3,16,8,128]{3,2,1,0:T(8,128)} copy(f32[3,16,8,128]{3,2,1,0:T(8,128)S(1)} %get-tuple-element.5) | data formatting | bytes 393216
Async XLA Ops:
  0.6 1.0 %copy-start.4 = (s32[16,8,128]{2,1,0:T(8,128)S(1)}, s32[16,8,128]{2,1,0:T(8,128)}, u32[]{:S(2)}) copy-start(s32[16,8,128]{2,1,0:T(8,128)} %counts_hbm.1) | copy-start | bytes 196612
  1.6 1.0 %copy-start = (f32[8,16,8,128]{3,2,1,0:T(8,128)S(1)}, f32[8,16,8,128]{3,2,1,0:T(8,128)}, u32[]{:S(2)}) copy-start(f32[8,16,8,128]{3,2,1,0:T(8,128)} %radius_hbm.1) | copy-start | bytes 1572868
  2.7 1.0 %copy-start.1 = (f32[8,16,8,128]{3,2,1,0:T(8,128)S(1)}, f32[8,16,8,128]{3,2,1,0:T(8,128)}, u32[]{:S(2)}) copy-start(f32[8,16,8,128]{3,2,1,0:T(8,128)} %weight_hbm.1) | copy-start | bytes 1572868
  3.7 1.0 %copy-start.2 = (s32[8,16,8,128]{3,2,1,0:T(8,128)S(1)}, s32[8,16,8,128]{3,2,1,0:T(8,128)}, u32[]{:S(2)}) copy-start(s32[8,16,8,128]{3,2,1,0:T(8,128)} %column_hbm.1) | copy-start | bytes 1572868
  4.7 1.0 %copy-start.3 = (f32[5,16,8,128]{3,2,1,0:T(8,128)S(1)}, f32[5,16,8,128]{3,2,1,0:T(8,128)}, u32[]{:S(2)}) copy-start(f32[5,16,8,128]{3,2,1,0:T(8,128)} %fields_hbm.1) | copy-start | bytes 983044
where the time goes:
time: 54.6 us; the launch traced here: 54.2 us
  Pallas kernels  47.1 us (86%)
  local copies, waits for them, and re-layouts  6.46 us (12%)
  between operations  0.67 us (1%)
    pallas_call x1, Pallas kernels, per_device(): pl.pallas_call(functools.partial(kernel, (tuple(spaces), levels, rows, co...  47.1 us
    unnamed x13, local copies, waits for them, and re-layouts  6.36 us

commit v1 on v0

v1 whole, which is shorter than its diff:
```python
import functools
import itertools
import jax
import jax.numpy as jnp
from jax import lax
from jax.experimental import pallas as pl
from jax.experimental.pallas import tpu as pltpu
from jax.sharding import PartitionSpec as P

NS = 4
FMAX = 8
CELLS = 8
SLOT = 8
EDGE = 3
CHUNKS = (24, 24, 16, 24, 8, 16, 16)
ONE_SHOT = 32

sound_speed = 10.0
buoyancy = 0.5
courant_goal = 0.6
growth = 0.3

MESH = pl.DeviceIdType.MESH
AXES = ("gy", "gx", "gz")
FULL = {"0": 0, "1": 1, "2": 2}
THIN = {"a": 0, "b": 1, "c": 2, "d": 3}


def flux(wind, a, b, c, d, e, f):
    central = 37.0 * (c + d) - 8.0 * (b + e) + (a + f)
    upwind = 10.0 * (d - c) - 5.0 * (e - b) + (f - a)
    return wind * central - jnp.abs(wind) * upwind


def max_groups(count):
    total = 1
    for a in AXES:
        total *= count[a]
    return (AXES,) if total <= ONE_SHOT else tuple((a,) for a in AXES)


def shifts_of(group, count):
    return [s for s in itertools.product(*(range(count[a]) for a in group)) if any(s)]


def kernel(
    sizes, depth_hbm, fields_hbm, radius_hbm, weight_hbm, column_hbm, counts_hbm,
    out_fields, moments, *scratch
):
    names, levels, rows, cols, slots = sizes
    refs = dict(zip(names, scratch))
    radius, weight, column, counts = (refs[n] for n in ("radius", "weight", "column", "counts"))
    depth = refs["depth"]
    vals, fallen = refs["vals"], refs["fallen"]
    local_sem = refs["local_sem"]
    shape = (rows, cols)
    lane = lax.broadcasted_iota(jnp.int32, shape, 1)
    row = lax.broadcasted_iota(jnp.int32, shape, 0)
    slot_lane = lane % SLOT
    place = {a: lax.axis_index(a) for a in AXES}
    count = {a: lax.axis_size(a) for a in AXES}
    groups = max_groups(count)
    has_low = place["gz"] > 0
    has_high = place["gz"] < count["gz"] - 1
    zero = jnp.zeros(shape, jnp.float32)

    def lanes_by(x, shift):
        return pltpu.roll(x, shift % cols, 1)

    def rows_by(x, shift):
        return pltpu.roll(x, shift % rows, 0)

    def loop(n, body, carry, unroll=True):
        return lax.fori_loop(0, n, body, carry, unroll=unroll)

    first_copies = []
    for n, dst in enumerate(
        (refs["C0"].at[pl.ds(3, levels)], refs["P0"].at[pl.ds(3, levels)],
         refs["U0"], refs["V0"], refs["W0"].at[pl.ds(1, levels)])
    ):
        first_copies.append(pltpu.make_async_copy(fields_hbm.at[n], dst, local_sem.at[n]))
    later_copies = []
    for n, (src, dst) in enumerate(
        ((counts_hbm, counts), (weight_hbm, weight), (radius_hbm, radius),
         (column_hbm, column), (depth_hbm, depth))
    ):
        later_copies.append(pltpu.make_async_copy(src, dst, local_sem.at[5 + n]))
    for copy in first_copies + later_copies:
        copy.start()

    def away(group, shift):
        return {a: lax.rem(place[a] + s, count[a]) for a, s in zip(group, shift) if s}

    barrier = pltpu.get_barrier_semaphore()
    peers = 0
    for group in groups:
        for shift in shifts_of(group, count):
            pl.semaphore_signal(barrier, inc=1, device_id=away(group, shift), device_id_type=MESH)
            peers += 1

    for copy in first_copies:
        copy.wait()

    @pl.when(jnp.logical_not(has_high))
    def _():
        refs["W0"][levels] = zero
        for tag in ("0", "1", "2"):
            for t in range(EDGE):
                refs["C" + tag][3 + levels + t] = zero
        for tag in "012abcd":
            for t in range(EDGE if tag in FULL else 1):
                refs["P" + tag][3 + levels + t] = zero

    @pl.when(jnp.logical_not(has_low))
    def _():
        refs["W0"][0] = zero
        for tag in ("0", "1", "2"):
            for t in range(EDGE):
                refs["C" + tag][t] = zero
        for tag in "012abcd":
            for t in range(3 - (EDGE if tag in FULL else 1), 3):
                refs["P" + tag][t] = zero

    def fastest(k, top):
        speed = jnp.abs(refs["U0"][k]) + jnp.abs(refs["V0"][k]) + jnp.abs(refs["W0"][k + 1])
        return jnp.maximum(top, speed)

    top = loop(levels, fastest, zero)
    top = jnp.max(top, axis=0, keepdims=True)
    pl.semaphore_wait(barrier, peers)

    def max_start(g, value):
        refs["max_send"][g] = value
        copies = []
        for n, shift in enumerate(shifts_of(groups[g], count)):
            copy = pltpu.make_async_remote_copy(
                src_ref=refs["max_send"].at[g],
                dst_ref=refs["max_recv"].at[g, n],
                send_sem=refs["max_ss"].at[g, n],
                recv_sem=refs["max_rs"].at[g, n],
                device_id=away(groups[g], shift), device_id_type=MESH,
            )
            copy.start()
            copies.append(copy)
        return copies

    def max_end(g, value, copies):
        for copy in copies:
            copy.wait()
        for n in range(len(copies)):
            value = jnp.maximum(value, refs["max_recv"][g, n])
        return value

    def neighbour(a, step):
        return {a: lax.rem(place[a] + count[a] + step, count[a])}

    def remote(src, dst, sems, n, a, step):
        return pltpu.make_async_remote_copy(
            src_ref=src, dst_ref=dst, send_sem=refs[sems + "_ss"].at[n],
            recv_sem=refs[sems + "_rs"].at[n],
            device_id=neighbour(a, step), device_id_type=MESH,
        )

    def y_copies(name, tag, sems, at):
        source = refs[name + tag]
        if tag in FULL:
            w, low, high, dst = EDGE, rows - EDGE, 0, refs["HY" + name + tag]
        else:
            w, low, high, dst = 1, 0, rows - 1, refs["HYT" + tag]
        own = pl.ds(3, levels)
        return (
            remote(source.at[own, pl.ds(rows - w, w), :], dst.at[:, pl.ds(low, w), :],
                   sems, at, "gy", 1),
            remote(source.at[own, pl.ds(0, w), :], dst.at[:, pl.ds(high, w), :],
                   sems, at + 1, "gy", -1),
        )

    def z_copies(name, tag, sems, at):
        w = EDGE if tag in FULL else 1
        q = refs[name + tag]
        return (
            remote(q.at[pl.ds(3 + levels - w, w)], q.at[pl.ds(3 - w, w)], sems, at, "gz", 1),
            remote(q.at[pl.ds(3, w)], q.at[pl.ds(3 + levels, w)], sems, at + 1, "gz", -1),
        )

    def x_copies(tag, sems, at):
        kind, e = ("fx", FULL[tag]) if tag in FULL else ("tx", THIN[tag])
        return (
            remote(refs[kind + "_s"].at[e], refs[kind + "_lo"].at[e], sems, at, "gx", 1),
            remote(refs[kind + "_s"].at[e], refs[kind + "_hi"].at[e], sems, at + 1, "gx", -1),
        )

    def z_start(pair):
        @pl.when(has_high)
        def _():
            pair[0].start()

        @pl.when(has_low)
        def _():
            pair[1].start()

    def z_wait(pair):
        @pl.when(has_high)
        def _():
            pair[0].wait_send()
            pair[1].wait_recv()

        @pl.when(has_low)
        def _():
            pair[1].wait_send()
            pair[0].wait_recv()

    def wind_copies():
        own = refs["V0"].at[:, pl.ds(rows - 1, 1), :]
        return (
            remote(own, refs["HYV0"].at[:, pl.ds(0, 1), :], "f0", 10, "gy", 1),
            remote(refs["W0"].at[levels], refs["W0"].at[0], "f0", 11, "gz", 1),
        )

    def pack(names_at, tag):
        def body(k, packed):
            out = []
            for name, got in zip(names_at, packed):
                edge = lanes_by(refs[name + tag][k + 3], SLOT * k + (EDGE if tag in FULL else 1))
                if tag == "0" and name == "P":
                    edge = jnp.where(
                        slot_lane == 6, lanes_by(refs["U0"][k], SLOT * k + 7), edge
                    )
                out.append(jnp.where(lane // SLOT == k, edge, got))
            return tuple(out)

        packed = (zero,) * len(names_at)
        for k in range(levels):
            packed = body(k, packed)
        return packed

    def send_full(tag):
        sems, e = "f" + tag, FULL[tag]
        x = x_copies(tag, sems, 0)
        for n, part in enumerate(pack("PC", tag)):
            refs["fx_s"][e, n] = part
        for copy in y_copies("P", tag, sems, 2):
            copy.start()
        if tag == "0":
            wind_copies()[0].start()
        for name, at in (("P", 4), ("C", 6)):
            z_start(z_copies(name, tag, sems, at))
        if tag == "0":
            @pl.when(has_high)
            def _():
                wind_copies()[1].start()
        for copy in x:
            copy.start()
        for copy in y_copies("C", tag, sems, 8):
            copy.start()

    def receive_xz(tag):
        sems, e = "f" + tag, FULL[tag]
        for copy in x_copies(tag, sems, 0):
            copy.wait()
        for n, name in enumerate("PC"):
            low, high = refs["fx_lo"][e, n], refs["fx_hi"][e, n]
            both = jnp.where(slot_lane < EDGE, low, high)
            for k in range(levels):
                refs["HX" + name + tag][k] = lanes_by(both, -(SLOT * k + EDGE))
            if tag == "0" and name == "P":
                for k in range(levels):
                    refs["HXU0"][k] = lanes_by(low, -(SLOT * k + 6))
        for name, at in (("P", 4), ("C", 6)):
            z_wait(z_copies(name, tag, sems, at))
        if tag == "0":
            @pl.when(has_high)
            def _():
                wind_copies()[1].wait_send()

            @pl.when(has_low)
            def _():
                wind_copies()[1].wait_recv()

    def receive_y(name, tag):
        for copy in y_copies(name, tag, "f" + tag, 2 if name == "P" else 8):
            copy.wait()
        if tag == "0" and name == "P":
            wind_copies()[0].wait()

    def first_edges():
        for k in range(levels):
            x, y = refs["HXP0"][k], refs["HYP0"][k]
            refs["HXT0"][k] = jnp.where(lane == 0, lanes_by(x, 1), lanes_by(x, -1))
            refs["HYT0"][k] = jnp.where(row == 0, rows_by(y, 1), rows_by(y, -1))

    def send_thin(tag):
        sems = "t" + tag
        refs["tx_s"][THIN[tag]] = pack("P", tag)[0]
        for copy in y_copies("P", tag, sems, 2):
            copy.start()
        z_start(z_copies("P", tag, sems, 4))
        for copy in x_copies(tag, sems, 0):
            copy.start()

    def receive_thin(tag):
        sems, e = "t" + tag, THIN[tag]
        for copy in x_copies(tag, sems, 0):
            copy.wait()
        low, high = refs["tx_lo"][e], refs["tx_hi"][e]
        both = jnp.where(slot_lane == 1, lanes_by(low, 1), lanes_by(high, -1))
        for k in range(levels):
            refs["HXT" + tag][k] = lanes_by(both, -(SLOT * k + 1))
        z_wait(z_copies("P", tag, sems, 4))
        for copy in y_copies("P", tag, sems, 2):
            copy.wait()

    def sides(q, halo, by, index, extent):
        low = [by(jnp.where(index >= extent - n, halo, q), n) for n in (3, 2, 1)]
        high = [by(jnp.where(index < n, halo, q), -n) for n in (1, 2, 3)]
        return (*low, q, *high)

    def advect_xz(name, tag, rate):
        Q, HX = refs[name + tag], refs["HX" + name + tag]

        def level(k, below):
            u = refs["U" + tag][k]
            u_low = jnp.where(lane == 0, refs["HXU" + tag][k], lanes_by(u, 1))
            xs = sides(Q[k + 3], HX[k], lanes_by, lane, cols)
            above = flux(refs["W" + tag][k + 1], *(Q[k + n] for n in range(1, 7)))
            total = flux(u, *xs[1:]) - flux(u_low, *xs[:6])
            refs[rate][k] = total + (above - below)
            return above

        loop(levels, level, flux(refs["W" + tag][0], *(Q[n] for n in range(6))))

    def advect_y(name, tag, rate):
        Q, HY = refs[name + tag], refs["HY" + name + tag]

        def level(k, carry):
            v = refs["V" + tag][k]
            v_low = jnp.where(row == 0, refs["HYV" + tag][k], rows_by(v, 1))
            ys = sides(Q[k + 3], HY[k], rows_by, row, rows)
            total = refs[rate][k] + (flux(v, *ys[1:]) - flux(v_low, *ys[:6]))
            refs[rate][k] = total * (-1.0 / 60.0)
            return carry

        loop(levels, level, 0)

    def lift_of(tag):
        C = refs["C" + tag]
        lid_low = jnp.where(has_low, 1.0, 0.0)
        lid_high = jnp.where(has_high, 1.0, 0.0)
        for k in range(levels + 1):
            lift = (buoyancy * 0.5) * (C[k + 2] + C[k + 3])
            if k == 0:
                lift = lift * lid_low
            if k == levels:
                lift = lift * lid_high
            refs["lift"][k] = lift

    def substep(sp, sw, dp, dw, sub_step):
        SP, HXT, HYT = refs["P" + sp], refs["HXT" + sp], refs["HYT" + sp]
        SU, SV, SW, HXU, HYV = (refs[n + sw] for n in ("U", "V", "W", "HXU", "HYV"))
        push = sub_step * sound_speed
        lid_low = jnp.where(has_low, 1.0, 0.0)
        lid_high = jnp.where(has_high, 1.0, 0.0)
        last = dp is None

        def vertical(k):
            return SW[k] + sub_step * (
                refs["lift"][k] - sound_speed * (SP[k + 3] - SP[k + 2])
            )

        w_low = vertical(0) * lid_low
        if not last:
            refs["W" + dw][0] = w_low
        for k in range(levels):
            p, u, v = SP[k + 3], SU[k], SV[k]
            hx, hy = HXT[k], HYT[k]
            w = vertical(k + 1)
            if k == levels - 1:
                w = w * lid_high
            u_new = u - push * (jnp.where(lane == cols - 1, hx, lanes_by(p, -1)) - p)
            v_new = v - push * (jnp.where(row == rows - 1, hy, rows_by(p, -1)) - p)
            u_halo = HXU[k] - push * (p - hx)
            v_halo = HYV[k] - push * (p - hy)
            u_low = jnp.where(lane == 0, u_halo, lanes_by(u_new, 1))
            v_low = jnp.where(row == 0, v_halo, rows_by(v_new, 1))
            div = (u_new - u_low) + (v_new - v_low) + (w - w_low)
            p_new = p + sub_step * (refs["rate_p"][k] - sound_speed * div)
            w_low = w
            if last:
                for n, part in enumerate((p_new, u_new, v_new, w)):
                    out_fields[n + 1, k] = part
            else:
                refs["U" + dw][k] = u_new
                refs["V" + dw][k] = v_new
                refs["W" + dw][k + 1] = w
                refs["HXU" + dw][k] = u_halo
                refs["HYV" + dw][k] = v_halo
                refs["P" + dp][k + 3] = p_new

    def tracer(tag, scale):
        for k in range(levels):
            value = refs["C0"][k + 3] + scale * refs["rate_c"][k]
            if tag is None:
                out_fields[0, k] = value
                swell = jnp.exp(growth * value)
                refs["swell"][0, k] = swell
                refs["swell"][1, k] = swell * jnp.sqrt(swell)
            else:
                refs["C" + tag][k + 3] = value

    def droplet_terms():
        for copy in later_copies:
            copy.wait()

        def cell(k, carry):
            live = counts[k]
            for s in range(slots):
                r = jnp.abs(radius[s, k])
                number = jnp.where(live > s, weight[s, k], 0.0)
                area = number * (r * r)
                mass = area * r
                for m, term in enumerate((number, area, mass)):
                    high = term.astype(jnp.bfloat16).astype(jnp.float32)
                    vals[s, k, m * rows:(m + 1) * rows, :] = high
                    vals[s, k, (m + 3) * rows:(m + 4) * rows, :] = term - high
                vals[s, k, 6 * rows:, :] = jnp.zeros((2 * rows, cols), jnp.float32)
            return carry

        loop(levels, cell, 0, 2)

    def deposit(begin, cells):
        ids = lax.broadcasted_iota(jnp.int32, (cols, cols), 0).astype(jnp.float32).astype(jnp.bfloat16)
        one = jnp.ones((cols, cols), jnp.bfloat16)
        none = jnp.zeros((cols, cols), jnp.bfloat16)
        blank = jnp.zeros((8, cols), jnp.float32)

        def cell(n, carry):
            k, j = (begin + n) // rows, (begin + n) % rows
            by_depth = [None] * (FMAX + 1)
            for s in range(0, slots, 4):
                left, hots = [], []
                for t in range(4):
                    v = vals[s + t, k, pl.ds(j, 8, stride=rows), :]
                    left.append(jnp.concatenate([v, blank] if t % 2 == 0 else [blank, v], axis=1))
                    c = column[s + t, k, pl.ds(j, 1), :].astype(jnp.float32).astype(jnp.bfloat16)
                    hots.append(jnp.where(ids == jnp.broadcast_to(c, (cols, cols)), one, none))
                lhs = jnp.concatenate(left, axis=0).astype(jnp.bfloat16)
                rhs = jnp.concatenate(
                    [jnp.concatenate(hots[:2], axis=1), jnp.concatenate(hots[2:], axis=1)], axis=0
                )
                got = lax.dot_general(
                    lhs, rhs, (((1,), (1,)), ((), ())), preferred_element_type=jnp.float32
                )
                for t in range(4):
                    half = t // 2
                    part = got[8 * t:8 * (t + 1), half * cols:(half + 1) * cols]
                    fall = depth[s + t, j, 0, k]
                    for d in range(FMAX + 1):
                        term = jnp.where(fall == d, part, 0.0)
                        by_depth[d] = term if by_depth[d] is None else by_depth[d] + term
            at = pl.ds(pl.multiple_of(j * 8, 8), 8)
            for d in range(FMAX + 1):
                fallen[k, d, at, :] = by_depth[d]
            return carry

        lax.fori_loop(0, cells, cell, 0, unroll=min(CELLS, cells))

    def landed(m, l):
        total = None
        for d in range(FMAX + 1):
            k = l + d
            if not 0 <= k < levels:
                continue
            part = (
                fallen[k, d, pl.ds(m, rows, stride=8), :]
                + fallen[k, d, pl.ds(m + 3, rows, stride=8), :]
            )
            if m:
                part = part * refs["swell"][m - 1, k]
            total = part if total is None else total + part
        return total

    def fall_copy(m):
        return remote(refs["fall_s"].at[m], refs["fall_r"].at[m], "fall", m, "gz", -1)

    def fall_send(m):
        for l in range(FMAX):
            refs["fall_s"][m, l] = landed(m, l - FMAX)

        @pl.when(has_low)
        def _():
            fall_copy(m).start()

    def fall_home(m):
        for l in range(levels):
            moments[m, l] = landed(m, l)

    begins = [sum(CHUNKS[:n]) for n in range(len(CHUNKS))]
    cells = levels * rows

    def chunk(n):
        begin = min(begins[n], cells)
        end = cells if n == len(CHUNKS) - 1 else min(begins[n] + CHUNKS[n], cells)
        if end > begin:
            deposit(begin, end - begin)

    copies = max_start(0, top)
    send_full("0")
    droplet_terms()
    receive_xz("0")
    receive_y("P", "0")
    receive_y("C", "0")
    first_edges()
    lift_of("0")
    for name, rate in (("P", "rate_p"), ("C", "rate_c")):
        advect_xz(name, "0", rate)
        advect_y(name, "0", rate)
    for g in range(1, len(groups)):
        top = max_end(g - 1, top, copies)
        copies = max_start(g, top)
    chunk(0)
    top = max_end(len(groups) - 1, top, copies)
    time_step = courant_goal / (1.0 + jnp.max(top, axis=(0, 1), keepdims=True))
    time_step = jnp.broadcast_to(time_step, shape)

    def section(tag, part, after):
        receive_xz(tag)
        lift_of(tag)
        advect_xz("P", tag, "rate_p")
        receive_y("P", tag)
        advect_y("P", tag, "rate_p")
        substep("0", "0", after, after, part)
        send_thin(after)
        receive_y("C", tag)
        advect_xz("C", tag, "rate_c")
        advect_y("C", tag, "rate_c")

    third = time_step * (1.0 / 3.0)
    tracer("1", third)
    substep("0", "0", "1", "1", third)
    send_full("1")
    chunk(1)
    half = time_step * 0.5
    part = half / (NS // 2)
    section("1", part, "a")
    tracer("2", half)
    chunk(2)
    receive_thin("a")
    substep("a", "a", "2", "2", part)
    send_full("2")
    chunk(3)
    fall_send(0)
    part = time_step / NS
    section("2", part, "b")
    tracer(None, time_step)
    fall_send(1)
    fall_send(2)
    chunk(4)
    receive_thin("b")
    substep("b", "b", "c", "b", part)
    send_thin("c")
    chunk(5)
    receive_thin("c")
    substep("c", "b", "d", "b", part)
    send_thin("d")
    chunk(6)
    for m in range(3):
        fall_home(m)
    receive_thin("d")
    substep("d", "b", None, None, part)

    @pl.when(has_low)
    def _():
        for m in range(3):
            fall_copy(m).wait_send()

    @pl.when(has_high)
    def _():
        for m in range(3):
            fall_copy(m).wait_recv()
            for l in range(FMAX):
                at = levels - FMAX + l
                moments[m, at] = moments[m, at] + refs["fall_r"][m, l]


def per_device(fields, radius, weight, column, counts, fall_depth):
    levels, rows, cols = fields.shape[1:]
    slots = radius.shape[0]
    assert slots % 4 == 0 and levels * SLOT <= cols and rows == 8 and FMAX <= levels
    f32 = jnp.float32
    cell = (rows, cols)
    count = {a: lax.axis_size(a) for a in AXES}
    groups = max_groups(count)
    widest = max(len(shifts_of(g, count)) for g in groups)
    spaces = {}

    def add(name, *shape, dtype=f32):
        spaces[name] = pltpu.VMEM(shape, dtype)

    add("radius", *radius.shape)
    add("weight", *weight.shape)
    add("column", *column.shape, dtype=jnp.int32)
    add("counts", *counts.shape, dtype=jnp.int32)
    spaces["depth"] = pltpu.SMEM((slots, rows, 1, levels), jnp.int32)
    for tag in "012":
        add("C" + tag, levels + 6, *cell)
        for name in ("HXC", "HXP", "HYC", "HYP"):
            add(name + tag, levels, *cell)
    for tag in "012abcd":
        add("P" + tag, levels + 6, *cell)
    for tag in "0abcd":
        add("HXT" + tag, levels, *cell)
        add("HYT" + tag, levels, *cell)
    for tag in "012ab":
        for name in ("U", "V", "HXU", "HYV"):
            add(name + tag, levels, *cell)
        add("W" + tag, levels + 1, *cell)
    add("rate_c", levels, *cell)
    add("rate_p", levels, *cell)
    add("lift", levels + 1, *cell)
    add("swell", 2, levels, *cell)
    add("max_send", len(groups), 1, cols)
    add("max_recv", len(groups), widest, 1, cols)
    for end in ("_s", "_lo", "_hi"):
        add("fx" + end, len(FULL), 2, *cell)
        add("tx" + end, len(THIN), *cell)
    add("vals", slots, levels, 8 * rows, cols)
    add("fallen", levels, FMAX + 1, 8 * rows, cols)
    add("fall_s", 3, FMAX, *cell)
    add("fall_r", 3, FMAX, *cell)
    for end in ("_ss", "_rs"):
        for tag in FULL:
            spaces["f" + tag + end] = pltpu.SemaphoreType.DMA((12,))
        for tag in THIN:
            spaces["t" + tag + end] = pltpu.SemaphoreType.DMA((6,))
        spaces["fall" + end] = pltpu.SemaphoreType.DMA((3,))
        spaces["max" + end] = pltpu.SemaphoreType.DMA((len(groups), widest))
    spaces["local_sem"] = pltpu.SemaphoreType.DMA((10,))
    vmem = pl.BlockSpec(memory_space=pltpu.VMEM)
    anywhere = pl.BlockSpec(memory_space=pltpu.HBM)
    return pl.pallas_call(
        functools.partial(kernel, (tuple(spaces), levels, rows, cols, slots)),
        out_shape=(
            jax.ShapeDtypeStruct(fields.shape, f32),
            jax.ShapeDtypeStruct((3, levels, rows, cols), f32),
        ),
        in_specs=[anywhere] * 6,
        out_specs=(vmem, vmem),
        scratch_shapes=list(spaces.values()),
        compiler_params=pltpu.CompilerParams(
            collective_id=0, has_side_effects=True, vmem_limit_bytes=67043328
        ),
        name="slab_step",
    )(fall_depth.transpose(0, 2, 3, 1), fields, radius, weight, column, counts)


def solution(mesh):
    in_specs = (
        P(None, "gz", "gy", "gx"),
        P(None, "gz", "gy", "gx"),
        P(None, "gz", "gy", "gx"),
        P(None, "gz", "gy", "gx"),
        P("gz", "gy", "gx"),
        P(None, "gz", "gy", "gx"),
    )
    out_specs = (P(None, "gz", "gy", "gx"), P(None, "gz", "gy", "gx"))
    return jax.shard_map(
        per_device, mesh=mesh, in_specs=in_specs, out_specs=out_specs, check_vma=False
    )
```

time: 54.6 us -> 40.1 us (0.73)
  Pallas kernels: 47.1 us -> 36.9 us
  local copies, waits for them, and re-layouts: 6.46 us -> 2.44 us
    pallas_call x1, Pallas kernels: 47.1 us -> 36.9 us  [per_device(): pl.pallas_call(functools.partial(kernel, (tuple(spaces), levels, rows, co...]
    unnamed x13 -> x4, local copies, waits for them, and re-layouts: 6.36 us -> 2.44 us
where the time goes in v1:
time: 40.1 us; the launch traced here: 39.9 us
  Pallas kernels  36.9 us (92%)
  local copies, waits for them, and re-layouts  2.44 us (6%)
  between operations  0.65 us (2%)
    pallas_call x1, Pallas kernels, per_device(): pl.pallas_call(functools.partial(kernel, (tuple(spaces), levels, rows, co...  36.9 us
    unnamed x4, local copies, waits for them, and re-layouts  2.44 us

profile of v1, /device:TPU:0, one launch (start us, length us, event | category | flops | bytes accessed | tf_op | source)
XLA Modules:
  0.0 39.9 jit_solution(382598647695056627)
XLA Ops:
  0.6 36.9 %slab_step.1 = (f32[5,16,8,128]{3,2,1,0:T(8,128)}, f32[3,16,8,128]{3,2,1,0:T(8,128)}) custom-call(s32[8,8,1,16]{3,2,1,0:T(1,128)} %bitcast.1, f32[5,16,8,128]{3,2,1,0:T(8,128)} %fields_hbm.1, f32[8,16,8,128]{3,2,1,0:T(8,128)} %radius_hbm.1, f32[8,16,8,128]{3,2,1,0:T(8,128)} %weight_hbm.1, s32[8,16,8,128]{3,2,1,0:T(8,128)} %column_hbm.1, s32[16,8,128]{2,1,0:T(8,128)} %counts_hbm.1), custom_call_target="tpu_custom_call" | custom-call | tf_op jit(solution)/shard_map/slab_step/pallas_call | solution.py:640
  37.5 0.0 copy-start
  37.5 1.8 %copy.10 = f32[5,16,8,128]{3,2,1,0:T(8,128)} copy(f32[5,16,8,128]{3,2,1,0:T(8,128)} %get-tuple-element.4) | data formatting | bytes 655360
  39.3 0.0 copy-done
  39.3 0.7 %copy.11 = f32[3,16,8,128]{3,2,1,0:T(8,128)} copy(f32[3,16,8,128]{3,2,1,0:T(8,128)S(1)} %copy-done) | data formatting | bytes 393216
Async XLA Ops:
  37.5 1.8 %copy-start = (f32[3,16,8,128]{3,2,1,0:T(8,128)S(1)}, f32[3,16,8,128]{3,2,1,0:T(8,128)}, u32[]{:S(2)}) copy-start(f32[3,16,8,128]{3,2,1,0:T(8,128)} %get-tuple-element.5) | copy-start | bytes 589828

commit v2 on v1

--- a/solution.py
+++ b/solution.py
@@ -14,6 +14,7 @@
 EDGE = 3
 CHUNKS = (24, 24, 16, 24, 8, 16, 16)
 ONE_SHOT = 32
+KERNEL_BYTES = 40 * 1024 * 1024
 
 sound_speed = 10.0
 buoyancy = 0.5
@@ -506,6 +507,15 @@
     copies = max_start(0, top)
     send_full("0")
     droplet_terms()
+    if len(groups) > 1:
+        chunk(0)
+        top = max_end(0, top, copies)
+        copies = max_start(1, top)
+        for g in range(2, len(groups)):
+            top = max_end(g - 1, top, copies)
+            copies = max_start(g, top)
+    else:
+        chunk(0)
     receive_xz("0")
     receive_y("P", "0")
     receive_y("C", "0")
@@ -514,10 +524,6 @@
     for name, rate in (("P", "rate_p"), ("C", "rate_c")):
         advect_xz(name, "0", rate)
         advect_y(name, "0", rate)
-    for g in range(1, len(groups)):
-        top = max_end(g - 1, top, copies)
-        copies = max_start(g, top)
-    chunk(0)
     top = max_end(len(groups) - 1, top, copies)
     time_step = courant_goal / (1.0 + jnp.max(top, axis=(0, 1), keepdims=True))
     time_step = jnp.broadcast_to(time_step, shape)
@@ -580,6 +586,17 @@
             for l in range(FMAX):
                 at = levels - FMAX + l
                 moments[m, at] = moments[m, at] + refs["fall_r"][m, l]
+
+
+def write_out(fields, moments, out_fields, out_moments, sem):
+    copies = [
+        pltpu.make_async_copy(fields, out_fields, sem.at[0]),
+        pltpu.make_async_copy(moments, out_moments, sem.at[1]),
+    ]
+    for copy in copies:
+        copy.start()
+    for copy in copies:
+        copy.wait()
 
 
 def per_device(fields, radius, weight, column, counts, fall_depth):
@@ -637,7 +654,7 @@
     spaces["local_sem"] = pltpu.SemaphoreType.DMA((10,))
     vmem = pl.BlockSpec(memory_space=pltpu.VMEM)
     anywhere = pl.BlockSpec(memory_space=pltpu.HBM)
-    return pl.pallas_call(
+    results = pl.pallas_call(
         functools.partial(kernel, (tuple(spaces), levels, rows, cols, slots)),
         out_shape=(
             jax.ShapeDtypeStruct(fields.shape, f32),
@@ -647,10 +664,23 @@
         out_specs=(vmem, vmem),
         scratch_shapes=list(spaces.values()),
         compiler_params=pltpu.CompilerParams(
-            collective_id=0, has_side_effects=True, vmem_limit_bytes=67043328
+            collective_id=0, has_side_effects=True,
+            vmem_limit_bytes=KERNEL_BYTES,
         ),
         name="slab_step",
-    )(fall_depth.transpose(0, 2, 3, 1), fields, radius, weight, column, counts)
+    )(*(
+        pltpu.with_memory_space_constraint(x, pltpu.HBM)
+        for x in (fall_depth.transpose(0, 2, 3, 1), fields, radius, weight, column, counts)
+    ))
+    return pl.pallas_call(
+        write_out,
+        out_shape=tuple(jax.ShapeDtypeStruct(r.shape, f32) for r in results),
+        in_specs=[vmem] * 2,
+        out_specs=(anywhere,) * 2,
+        scratch_shapes=[pltpu.SemaphoreType.DMA((2,))],
+        compiler_params=pltpu.CompilerParams(vmem_limit_bytes=1024 * 1024),
+        name="write_out",
+    )(*results)
 
 
 def solution(mesh):

time: 40.1 us -> 34.9 us (0.87)
  Pallas kernels: 36.9 us -> 34.1 us
  local copies, waits for them, and re-layouts: 2.44 us -> 0 us
    pallas_call x1, Pallas kernels: 36.9 us -> 33.3 us  [per_device(): pl.pallas_call(functools.partial(kernel, (tuple(spaces), levels, rows, co...]
    unnamed x4 -> x0, local copies, waits for them, and re-layouts: 2.44 us -> none
    pallas_call x0 -> x1, Pallas kernels: none -> 0.8 us  [per_device(): pl.pallas_call(write_out, out_shape=tuple((jax.ShapeDtypeStruct(r.shape,...]
where the time goes in v2:
time: 34.9 us; the launch traced here: 34.8 us
  Pallas kernels  34.1 us (98%)
  between operations  0.64 us (2%)
    pallas_call x1, Pallas kernels, per_device(): pl.pallas_call(functools.partial(kernel, (tuple(spaces), levels, rows, co...  33.3 us
    pallas_call x1, Pallas kernels, per_device(): pl.pallas_call(write_out, out_shape=tuple((jax.ShapeDtypeStruct(r.shape,...  0.8 us

profile of v2, /device:TPU:0, one launch (start us, length us, event | category | flops | bytes accessed | tf_op | source)
XLA Modules:
  0.0 34.8 jit_solution(13043712835643405802)
XLA Ops:
  0.6 33.3 %slab_step.1 = (f32[5,16,8,128]{3,2,1,0:T(8,128)S(1)}, f32[3,16,8,128]{3,2,1,0:T(8,128)S(1)}) custom-call(s32[8,8,1,16]{3,2,1,0:T(1,128)} %bitcast.1, f32[5,16,8,128]{3,2,1,0:T(8,128)} %fields_hbm.1, f32[8,16,8,128]{3,2,1,0:T(8,128)} %radius_hbm.1, f32[8,16,8,128]{3,2,1,0:T(8,128)} %weight_hbm.1, s32[8,16,8,128]{3,2,1,0:T(8,128)} %column_hbm.1, ...), custom_call_target="tpu_custom_call" | custom-call | tf_op jit(solution)/shard_map/slab_step/pallas_call | solution.py:657
  34.0 0.8 %write_out.1 = (f32[5,16,8,128]{3,2,1,0:T(8,128)}, f32[3,16,8,128]{3,2,1,0:T(8,128)}) custom-call(f32[5,16,8,128]{3,2,1,0:T(8,128)S(1)} %get-tuple-element.4.fields, f32[3,16,8,128]{3,2,1,0:T(8,128)S(1)} %get-tuple-element.5.moments), custom_call_target="tpu_custom_call" | custom-call | tf_op jit(solution)/shard_map/write_out/pallas_call | solution.py:675

commit v3 on v2

--- a/solution.py
+++ b/solution.py
@@ -12,7 +12,7 @@
 CELLS = 8
 SLOT = 8
 EDGE = 3
-CHUNKS = (24, 24, 16, 24, 8, 16, 16)
+CHUNKS = (32, 24, 28, 24, 20)
 ONE_SHOT = 32
 KERNEL_BYTES = 40 * 1024 * 1024
 
@@ -24,7 +24,8 @@
 MESH = pl.DeviceIdType.MESH
 AXES = ("gy", "gx", "gz")
 FULL = {"0": 0, "1": 1, "2": 2}
-THIN = {"a": 0, "b": 1, "c": 2, "d": 3}
+THIN = {"c": 0, "d": 1}
+DELTA = {"a": 0, "b": 1}
 
 
 def flux(wind, a, b, c, d, e, f):
@@ -42,6 +43,20 @@
 
 def shifts_of(group, count):
     return [s for s in itertools.product(*(range(count[a]) for a in group)) if any(s)]
+
+
+def greeted(groups, count):
+    found = {}
+    diagonals = [
+        (pair, steps)
+        for pair in itertools.combinations(AXES, 2)
+        for steps in itertools.product((1, -1), repeat=2)
+    ]
+    for group, shift in [(g, s) for g in groups for s in shifts_of(g, count)] + diagonals:
+        step = {a: s % count[a] for a, s in zip(group, shift) if s % count[a]}
+        if step:
+            found[tuple(sorted(step.items()))] = step
+    return list(found.values())
 
 
 def kernel(
@@ -94,10 +109,12 @@
 
     barrier = pltpu.get_barrier_semaphore()
     peers = 0
-    for group in groups:
-        for shift in shifts_of(group, count):
-            pl.semaphore_signal(barrier, inc=1, device_id=away(group, shift), device_id_type=MESH)
-            peers += 1
+    for step in greeted(groups, count):
+        pl.semaphore_signal(
+            barrier, inc=1, device_id=away(tuple(step), tuple(step.values())),
+            device_id_type=MESH,
+        )
+        peers += 1
 
     for copy in first_copies:
         copy.wait()
@@ -152,14 +169,17 @@
             value = jnp.maximum(value, refs["max_recv"][g, n])
         return value
 
-    def neighbour(a, step):
-        return {a: lax.rem(place[a] + count[a] + step, count[a])}
-
-    def remote(src, dst, sems, n, a, step):
+    def neighbour(*steps):
+        return {
+            a: lax.rem(place[a] + count[a] + step, count[a])
+            for a, step in zip(steps[::2], steps[1::2])
+        }
+
+    def remote(src, dst, sems, n, *steps):
         return pltpu.make_async_remote_copy(
             src_ref=src, dst_ref=dst, send_sem=refs[sems + "_ss"].at[n],
             recv_sem=refs[sems + "_rs"].at[n],
-            device_id=neighbour(a, step), device_id_type=MESH,
+            device_id=neighbour(*steps), device_id_type=MESH,
         )
 
     def y_copies(name, tag, sems, at):
@@ -184,105 +204,110 @@
             remote(q.at[pl.ds(3, w)], q.at[pl.ds(3 + levels, w)], sems, at + 1, "gz", -1),
         )
 
-    def x_copies(tag, sems, at):
-        kind, e = ("fx", FULL[tag]) if tag in FULL else ("tx", THIN[tag])
+    def x_copies(kind, e, sems, at):
         return (
             remote(refs[kind + "_s"].at[e], refs[kind + "_lo"].at[e], sems, at, "gx", 1),
             remote(refs[kind + "_s"].at[e], refs[kind + "_hi"].at[e], sems, at + 1, "gx", -1),
         )
 
-    def z_start(pair):
+    def start(copies):
+        for copy in copies:
+            copy.start()
+
+    def wait(copies):
+        for copy in copies:
+            copy.wait()
+
+    def z_start(up, down):
         @pl.when(has_high)
         def _():
-            pair[0].start()
+            start(up)
 
         @pl.when(has_low)
         def _():
-            pair[1].start()
-
-    def z_wait(pair):
+            start(down)
+
+    def z_wait(up, down):
         @pl.when(has_high)
         def _():
-            pair[0].wait_send()
-            pair[1].wait_recv()
+            for copy in up:
+                copy.wait_send()
+            for copy in down:
+                copy.wait_recv()
 
         @pl.when(has_low)
         def _():
-            pair[1].wait_send()
-            pair[0].wait_recv()
+            for copy in down:
+                copy.wait_send()
+            for copy in up:
+                copy.wait_recv()
 
     def wind_copies():
         own = refs["V0"].at[:, pl.ds(rows - 1, 1), :]
         return (
-            remote(own, refs["HYV0"].at[:, pl.ds(0, 1), :], "f0", 10, "gy", 1),
-            remote(refs["W0"].at[levels], refs["W0"].at[0], "f0", 11, "gz", 1),
+            remote(own, refs["HYV0"].at[:, pl.ds(0, 1), :], "f0", 12, "gy", 1),
+            remote(refs["W0"].at[levels], refs["W0"].at[0], "f0", 13, "gz", 1),
         )
 
-    def pack(names_at, tag):
-        def body(k, packed):
-            out = []
-            for name, got in zip(names_at, packed):
-                edge = lanes_by(refs[name + tag][k + 3], SLOT * k + (EDGE if tag in FULL else 1))
-                if tag == "0" and name == "P":
-                    edge = jnp.where(
-                        slot_lane == 6, lanes_by(refs["U0"][k], SLOT * k + 7), edge
-                    )
-                out.append(jnp.where(lane // SLOT == k, edge, got))
-            return tuple(out)
-
-        packed = (zero,) * len(names_at)
+    def pack(value, packed=None):
         for k in range(levels):
-            packed = body(k, packed)
+            edge = lanes_by(value(k), SLOT * k + EDGE)
+            packed = edge if packed is None else jnp.where(lane // SLOT == k, edge, packed)
         return packed
 
-    def send_full(tag):
+    def pairs(low, high):
+        return jnp.where(slot_lane == EDGE, lanes_by(low, 1), lanes_by(high, -1))
+
+    def to_level(packed, k):
+        return lanes_by(packed, -(SLOT * k + EDGE))
+
+    def send_full(name, tag):
         sems, e = "f" + tag, FULL[tag]
-        x = x_copies(tag, sems, 0)
-        for n, part in enumerate(pack("PC", tag)):
-            refs["fx_s"][e, n] = part
-        for copy in y_copies("P", tag, sems, 2):
-            copy.start()
-        if tag == "0":
-            wind_copies()[0].start()
-        for name, at in (("P", 4), ("C", 6)):
-            z_start(z_copies(name, tag, sems, at))
-        if tag == "0":
-            @pl.when(has_high)
-            def _():
-                wind_copies()[1].start()
-        for copy in x:
-            copy.start()
-        for copy in y_copies("C", tag, sems, 8):
-            copy.start()
-
-    def receive_xz(tag):
+        at = 0 if name == "P" else 6
+        packed = pack(lambda k: refs[name + tag][k + 3])
+        z = z_copies(name, tag, sems, at + 4)
+        if tag == "0" and name == "P":
+            for k in range(levels):
+                wind = lanes_by(refs["U0"][k], SLOT * k + 7)
+                packed = jnp.where((lane // SLOT == k) & (slot_lane == 6), wind, packed)
+        refs["x" + name + "_s"][e] = packed
+        if name == "P":
+            start(y_copies(name, tag, sems, at + 2))
+            if tag == "0":
+                start(wind_copies()[:1])
+                z_start((z[0], wind_copies()[1]), (z[1],))
+            else:
+                z_start((z[0],), (z[1],))
+            start(x_copies("x" + name, e, sems, at))
+        else:
+            z_start((z[0],), (z[1],))
+            start(x_copies("x" + name, e, sems, at))
+            start(y_copies(name, tag, sems, at + 2))
+
+    def receive_x(name, tag, fix=None):
         sems, e = "f" + tag, FULL[tag]
-        for copy in x_copies(tag, sems, 0):
-            copy.wait()
-        for n, name in enumerate("PC"):
-            low, high = refs["fx_lo"][e, n], refs["fx_hi"][e, n]
-            both = jnp.where(slot_lane < EDGE, low, high)
+        wait(x_copies("x" + name, e, sems, 0 if name == "P" else 6))
+        low, high = refs["x" + name + "_lo"][e], refs["x" + name + "_hi"][e]
+        both = jnp.where(slot_lane < EDGE, low, high)
+        if fix is not None:
+            both = both + fix
+        for k in range(levels):
+            refs["HX" + name + tag][k] = to_level(both, k)
+        if tag == "0" and name == "P":
             for k in range(levels):
-                refs["HX" + name + tag][k] = lanes_by(both, -(SLOT * k + EDGE))
-            if tag == "0" and name == "P":
-                for k in range(levels):
-                    refs["HXU0"][k] = lanes_by(low, -(SLOT * k + 6))
-        for name, at in (("P", 4), ("C", 6)):
-            z_wait(z_copies(name, tag, sems, at))
-        if tag == "0":
-            @pl.when(has_high)
-            def _():
-                wind_copies()[1].wait_send()
-
-            @pl.when(has_low)
-            def _():
-                wind_copies()[1].wait_recv()
+                refs["HXU0"][k] = lanes_by(low, -(SLOT * k + 6))
+
+    def receive_z(name, tag):
+        z = z_copies(name, tag, "f" + tag, 4 if name == "P" else 10)
+        if tag == "0" and name == "P":
+            z_wait((z[0], wind_copies()[1]), (z[1],))
+        else:
+            z_wait((z[0],), (z[1],))
 
     def receive_y(name, tag):
-        for copy in y_copies(name, tag, "f" + tag, 2 if name == "P" else 8):
-            copy.wait()
+        wait(y_copies(name, tag, "f" + tag, 2 if name == "P" else 8))
         if tag == "0" and name == "P":
-            wind_copies()[0].wait()
+            wait(wind_copies()[:1])
 
     def first_edges():
         for k in range(levels):
@@ -291,25 +316,141 @@
             refs["HYT0"][k] = jnp.where(row == 0, rows_by(y, 1), rows_by(y, -1))
 
     def send_thin(tag):
-        sems = "t" + tag
-        refs["tx_s"][THIN[tag]] = pack("P", tag)[0]
-        for copy in y_copies("P", tag, sems, 2):
-            copy.start()
-        z_start(z_copies("P", tag, sems, 4))
-        for copy in x_copies(tag, sems, 0):
-            copy.start()
-
-    def receive_thin(tag):
         sems, e = "t" + tag, THIN[tag]
-        for copy in x_copies(tag, sems, 0):
-            copy.wait()
+        z = z_copies("P", tag, sems, 4)
+        refs["tx_s"][e] = pack(lambda k: refs["P" + tag][k + 3])
+        start(y_copies("P", tag, sems, 2))
+        z_start((z[0],), (z[1],))
+        start(x_copies("tx", e, sems, 0))
+
+    def receive_thin(tag, fix=None):
+        sems, e = "t" + tag, THIN[tag]
+        z = z_copies("P", tag, sems, 4)
+        wait(x_copies("tx", e, sems, 0))
         low, high = refs["tx_lo"][e], refs["tx_hi"][e]
-        both = jnp.where(slot_lane == 1, lanes_by(low, 1), lanes_by(high, -1))
+        if fix is not None:
+            low, high = low + fix, high + fix
+        both = pairs(low, high)
         for k in range(levels):
-            refs["HXT" + tag][k] = lanes_by(both, -(SLOT * k + 1))
-        z_wait(z_copies("P", tag, sems, 4))
-        for copy in y_copies("P", tag, sems, 2):
-            copy.wait()
+            refs["HXT" + tag][k] = to_level(both, k)
+        z_wait((z[0],), (z[1],))
+        wait(y_copies("P", tag, sems, 2))
+
+    def change(tag, k):
+        return refs["P" + tag][k + 3] - refs["P0"][k + 3]
+
+    top_rows, low_rows = pl.ds(rows - EDGE, EDGE), pl.ds(0, EDGE)
+    top_levels, low_levels = pl.ds(EDGE, EDGE), pl.ds(0, EDGE)
+
+    def delta_copies(tag):
+        e, sems = DELTA[tag], "d" + tag
+        s, dz = refs["d_s"].at[e], refs["dz_s"].at[e]
+        flat = list(x_copies("d", e, sems, 0)) + list(y_copies("P", tag, sems, 2))
+        for n, (end, sx) in enumerate((("lo", 1), ("hi", -1))):
+            dst = refs["dxy_" + end].at[e]
+            for m, (part, sy) in enumerate(((top_rows, 1), (low_rows, -1))):
+                flat.append(remote(s.at[part, :], dst.at[part, :], sems, 6 + 2 * n + m,
+                                   "gx", sx, "gy", sy))
+        z = z_copies("P", tag, sems, 4)
+        ups, downs = [z[0]], [z[1]]
+        for t, (found, sz, part) in enumerate(((ups, 1, top_levels), (downs, -1, low_levels))):
+            for n, (end, sx) in enumerate((("lo", 1), ("hi", -1))):
+                found.append(remote(s, refs["dxz_" + end].at[e, t], sems, 10 + 2 * t + n,
+                                    "gx", sx, "gz", sz))
+            for n, (part_y, sy) in enumerate(((top_rows, 1), (low_rows, -1))):
+                found.append(remote(dz.at[part, part_y, :], refs["dyz"].at[e, t, :, part_y, :],
+                                    sems, 14 + 2 * t + n, "gy", sy, "gz", sz))
+        return flat, ups, downs
+
+    def send_delta(tag):
+        e = DELTA[tag]
+        for t in range(EDGE):
+            refs["dz_s"][e, t] = change(tag, t)
+            refs["dz_s"][e, EDGE + t] = change(tag, levels - EDGE + t)
+        refs["d_s"][e] = pack(lambda k: change(tag, k))
+        flat, ups, downs = delta_copies(tag)
+        z_start(ups, downs)
+        start(flat)
+
+    def receive_delta(tag):
+        flat, ups, downs = delta_copies(tag)
+        wait(flat)
+        z_wait(ups, downs)
+
+    edge_lane = (lane == 0) | (lane == cols - 1)
+    edge_row = (row == 0) | (row == rows - 1)
+
+    def nearer(x):
+        return jnp.where(row == 0, rows_by(x, 1), rows_by(x, -1))
+
+    def packed_fix(tag):
+        e = DELTA[tag]
+        d = refs["d_s"][e]
+        across = jnp.where(slot_lane < EDGE, refs["dxy_lo"][e], refs["dxy_hi"][e])
+        below = jnp.where(slot_lane < EDGE, refs["dxz_lo"][e, 0], refs["dxz_hi"][e, 0])
+        above = jnp.where(slot_lane < EDGE, refs["dxz_lo"][e, 1], refs["dxz_hi"][e, 1])
+        last = SLOT * (levels - 1)
+        fix = jnp.where(
+            slot_lane == EDGE - 1, lanes_by(d, -1),
+            jnp.where(slot_lane == EDGE, lanes_by(d, 1), 0.0),
+        )
+        fix = fix + jnp.where(edge_row, nearer(across), 0.0)
+        fix = fix + jnp.where((lane < SLOT) & has_low, lanes_by(below, -last), 0.0)
+        return fix + jnp.where((lane // SLOT == levels - 1) & has_high, lanes_by(above, last), 0.0)
+
+    def mend(tag, p_tag, w_tag, push):
+        e, gain = DELTA[tag], push * push
+        P, U, V, W, HXU, HYV = (refs[n] for n in (
+            "P" + p_tag, "U" + w_tag, "V" + w_tag, "W" + w_tag, "HXU" + w_tag, "HYV" + w_tag,
+        ))
+        full = p_tag in FULL
+        face = pairs(refs["d_lo"][e], refs["d_hi"][e])
+        corner = pairs(refs["dxy_lo"][e], refs["dxy_hi"][e])
+        low = refs["P" + tag][2] - refs["P0"][2]
+        high = refs["P" + tag][3 + levels] - refs["P0"][3 + levels]
+        W[0] = W[0] + push * low
+        W[levels] = W[levels] - push * high
+        for k in range(levels):
+            own = change(tag, k)
+            dx = jnp.where(edge_lane, to_level(face, k), 0.0)
+            dy = jnp.where(edge_row, refs["HYT" + tag][k] - refs["HYT0"][k], 0.0)
+            total = dx + dy
+            if k == 0:
+                total = total + low
+            if k == levels - 1:
+                total = total + high
+            P[k + 3] = P[k + 3] + gain * total
+            U[k] = U[k] - push * jnp.where(lane == cols - 1, dx, 0.0)
+            V[k] = V[k] - push * jnp.where(row == rows - 1, dy, 0.0)
+            HXU[k] = HXU[k] + push * dx
+            HYV[k] = HYV[k] + push * dy
+            beside = jnp.where(edge_row, jnp.where(row == 0, rows_by(own, 1), rows_by(own, -1)), 0.0)
+            beside = beside + jnp.where(edge_lane, to_level(corner, k), 0.0)
+            if k == 0:
+                beside = beside + jnp.where(has_low, refs["dyz"][e, 0, EDGE - 1], 0.0)
+            if k == levels - 1:
+                beside = beside + jnp.where(has_high, refs["dyz"][e, 1, 0], 0.0)
+            if full:
+                refs["HYP" + p_tag][k] = refs["HYP" + p_tag][k] + gain * beside
+            else:
+                refs["HYT" + p_tag][k] = refs["HYT" + p_tag][k] + gain * nearer(beside)
+
+        def layers(t, wanted, nearest, source, level, at):
+            sides_of = pairs(refs["dxz_lo"][e, t], refs["dxz_hi"][e, t])
+            for n in wanted:
+                part = jnp.where(edge_lane, to_level(sides_of, level + n), 0.0)
+                part = part + jnp.where(edge_row, nearer(refs["dyz"][e, t, n]), 0.0)
+                if n == nearest:
+                    part = part + change(tag, source)
+                P[at + n] = P[at + n] + gain * part
+
+        @pl.when(has_low)
+        def _():
+            layers(0, range(EDGE) if full else (EDGE - 1,), EDGE - 1, 0, levels - EDGE, 0)
+
+        @pl.when(has_high)
+        def _():
+            layers(1, range(EDGE) if full else (0,), 0, levels - 1, 0, 3 + levels)
 
     def sides(q, halo, by, index, extent):
         low = [by(jnp.where(index >= extent - n, halo, q), n) for n in (3, 2, 1)]
@@ -355,8 +496,8 @@
                 lift = lift * lid_high
             refs["lift"][k] = lift
 
-    def substep(sp, sw, dp, dw, sub_step):
-        SP, HXT, HYT = refs["P" + sp], refs["HXT" + sp], refs["HYT" + sp]
+    def substep(sp, hp, sw, dp, dw, sub_step):
+        SP, HP, HXT, HYT = refs["P" + sp], refs["P" + hp], refs["HXT" + hp], refs["HYT" + hp]
         SU, SV, SW, HXU, HYV = (refs[n + sw] for n in ("U", "V", "W", "HXU", "HYV"))
         push = sub_step * sound_speed
         lid_low = jnp.where(has_low, 1.0, 0.0)
@@ -364,9 +505,9 @@
         last = dp is None
 
         def vertical(k):
-            return SW[k] + sub_step * (
-                refs["lift"][k] - sound_speed * (SP[k + 3] - SP[k + 2])
-            )
+            above = (HP if k == levels else SP)[k + 3]
+            below = (HP if k == 0 else SP)[k + 2]
+            return SW[k] + sub_step * (refs["lift"][k] - sound_speed * (above - below))
 
         w_low = vertical(0) * lid_low
         if not last:
@@ -504,75 +645,90 @@
         if end > begin:
             deposit(begin, end - begin)
 
+    def advect(name, tag, rate):
+        advect_xz(name, tag, rate)
+        receive_y(name, tag)
+        advect_y(name, tag, rate)
+
+    def tracer_section(tag):
+        receive_x("C", tag)
+        advect("C", tag, "rate_c")
+
     copies = max_start(0, top)
-    send_full("0")
+    send_full("P", "0")
+    send_full("C", "0")
     droplet_terms()
-    if len(groups) > 1:
-        chunk(0)
-        top = max_end(0, top, copies)
-        copies = max_start(1, top)
-        for g in range(2, len(groups)):
-            top = max_end(g - 1, top, copies)
-            copies = max_start(g, top)
-    else:
-        chunk(0)
-    receive_xz("0")
-    receive_y("P", "0")
-    receive_y("C", "0")
+    chunk(0)
+    for g in range(1, len(groups)):
+        top = max_end(g - 1, top, copies)
+        copies = max_start(g, top)
+    receive_x("P", "0")
+    receive_z("P", "0")
+    advect("P", "0", "rate_p")
     first_edges()
+    receive_z("C", "0")
     lift_of("0")
-    for name, rate in (("P", "rate_p"), ("C", "rate_c")):
-        advect_xz(name, "0", rate)
-        advect_y(name, "0", rate)
     top = max_end(len(groups) - 1, top, copies)
     time_step = courant_goal / (1.0 + jnp.max(top, axis=(0, 1), keepdims=True))
     time_step = jnp.broadcast_to(time_step, shape)
 
-    def section(tag, part, after):
-        receive_xz(tag)
-        lift_of(tag)
-        advect_xz("P", tag, "rate_p")
-        receive_y("P", tag)
-        advect_y("P", tag, "rate_p")
-        substep("0", "0", after, after, part)
-        send_thin(after)
-        receive_y("C", tag)
-        advect_xz("C", tag, "rate_c")
-        advect_y("C", tag, "rate_c")
-
     third = time_step * (1.0 / 3.0)
+    substep("0", "0", "0", "1", "1", third)
+    send_full("P", "1")
+    tracer_section("0")
     tracer("1", third)
-    substep("0", "0", "1", "1", third)
-    send_full("1")
+    send_full("C", "1")
     chunk(1)
+
+    receive_x("P", "1")
+    receive_z("P", "1")
+    advect("P", "1", "rate_p")
+    receive_z("C", "1")
+    lift_of("1")
     half = time_step * 0.5
     part = half / (NS // 2)
-    section("1", part, "a")
+    substep("0", "0", "0", "a", "a", part)
+    send_delta("a")
+    substep("a", "0", "a", "2", "2", part)
+    send_full("P", "2")
+    tracer_section("1")
     tracer("2", half)
+    send_full("C", "2")
     chunk(2)
-    receive_thin("a")
-    substep("a", "a", "2", "2", part)
-    send_full("2")
-    chunk(3)
     fall_send(0)
+
+    receive_delta("a")
+    push = part * sound_speed
+    receive_x("P", "2", push * push * packed_fix("a"))
+    receive_z("P", "2")
+    receive_y("P", "2")
+    mend("a", "2", "2", push)
+    advect_xz("P", "2", "rate_p")
+    advect_y("P", "2", "rate_p")
+    receive_z("C", "2")
+    lift_of("2")
     part = time_step / NS
-    section("2", part, "b")
+    substep("0", "0", "0", "b", "b", part)
+    send_delta("b")
+    substep("b", "0", "b", "c", "c", part)
+    send_thin("c")
+    tracer_section("2")
     tracer(None, time_step)
     fall_send(1)
     fall_send(2)
+    chunk(3)
+
+    receive_delta("b")
+    push = part * sound_speed
+    receive_thin("c", push * push * packed_fix("b"))
+    mend("b", "c", "c", push)
+    substep("c", "c", "c", "d", "c", part)
+    send_thin("d")
     chunk(4)
-    receive_thin("b")
-    substep("b", "b", "c", "b", part)
-    send_thin("c")
-    chunk(5)
-    receive_thin("c")
-    substep("c", "b", "d", "b", part)
-    send_thin("d")
-    chunk(6)
     for m in range(3):
         fall_home(m)
     receive_thin("d")
-    substep("d", "b", None, None, part)
+    substep("d", "d", "c", None, None, part)
 
     @pl.when(has_low)
     def _():
@@ -602,7 +758,7 @@
 def per_device(fields, radius, weight, column, counts, fall_depth):
     levels, rows, cols = fields.shape[1:]
     slots = radius.shape[0]
-    assert slots % 4 == 0 and levels * SLOT <= cols and rows == 8 and FMAX <= levels
+    assert slots % 4 == 0 and levels * SLOT <= cols and rows == 8 and max(FMAX, 2 * EDGE) <= levels
     f32 = jnp.float32
     cell = (rows, cols)
     count = {a: lax.axis_size(a) for a in AXES}
@@ -624,10 +780,11 @@
             add(name + tag, levels, *cell)
     for tag in "012abcd":
         add("P" + tag, levels + 6, *cell)
+    for tag in "0cd":
+        add("HXT" + tag, levels, *cell)
     for tag in "0abcd":
-        add("HXT" + tag, levels, *cell)
         add("HYT" + tag, levels, *cell)
-    for tag in "012ab":
+    for tag in "012abc":
         for name in ("U", "V", "HXU", "HYV"):
             add(name + tag, levels, *cell)
         add("W" + tag, levels + 1, *cell)
@@ -638,17 +795,26 @@
     add("max_send", len(groups), 1, cols)
     add("max_recv", len(groups), widest, 1, cols)
     for end in ("_s", "_lo", "_hi"):
-        add("fx" + end, len(FULL), 2, *cell)
+        add("xP" + end, len(FULL), *cell)
+        add("xC" + end, len(FULL), *cell)
         add("tx" + end, len(THIN), *cell)
+        add("d" + end, len(DELTA), *cell)
+    for end in ("_lo", "_hi"):
+        add("dxy" + end, len(DELTA), *cell)
+        add("dxz" + end, len(DELTA), 2, *cell)
+    add("dz_s", len(DELTA), 2 * EDGE, *cell)
+    add("dyz", len(DELTA), 2, EDGE, *cell)
     add("vals", slots, levels, 8 * rows, cols)
     add("fallen", levels, FMAX + 1, 8 * rows, cols)
     add("fall_s", 3, FMAX, *cell)
     add("fall_r", 3, FMAX, *cell)
     for end in ("_ss", "_rs"):
         for tag in FULL:
-            spaces["f" + tag + end] = pltpu.SemaphoreType.DMA((12,))
+            spaces["f" + tag + end] = pltpu.SemaphoreType.DMA((14,))
         for tag in THIN:
             spaces["t" + tag + end] = pltpu.SemaphoreType.DMA((6,))
+        for tag in DELTA:
+            spaces["d" + tag + end] = pltpu.SemaphoreType.DMA((18,))
         spaces["fall" + end] = pltpu.SemaphoreType.DMA((3,))
         spaces["max" + end] = pltpu.SemaphoreType.DMA((len(groups), widest))
     spaces["local_sem"] = pltpu.SemaphoreType.DMA((10,))

time: 34.9 us -> 33.7 us (0.966)
  Pallas kernels: 34.1 us -> 32.9 us
    pallas_call x1, Pallas kernels: 33.3 us -> 32.1 us  [per_device(): pl.pallas_call(functools.partial(kernel, (tuple(spaces), levels, rows, co...]
where the time goes in v3:
time: 33.7 us; the launch traced here: 33.6 us
  Pallas kernels  32.9 us (98%)
  between operations  0.64 us (2%)
    pallas_call x1, Pallas kernels, per_device(): pl.pallas_call(functools.partial(kernel, (tuple(spaces), levels, rows, co...  32.1 us
    pallas_call x1, Pallas kernels, per_device(): pl.pallas_call(write_out, out_shape=tuple((jax.ShapeDtypeStruct(r.shape,...  0.8 us

profile of v3, /device:TPU:0, one launch (start us, length us, event | category | flops | bytes accessed | tf_op | source)
XLA Modules:
  0.0 33.6 jit_solution(17369413995622266860)
XLA Ops:
  0.6 32.1 %slab_step.1 = (f32[5,16,8,128]{3,2,1,0:T(8,128)S(1)}, f32[3,16,8,128]{3,2,1,0:T(8,128)S(1)}) custom-call(s32[8,8,1,16]{3,2,1,0:T(1,128)} %bitcast.1, f32[5,16,8,128]{3,2,1,0:T(8,128)} %fields_hbm.1, f32[8,16,8,128]{3,2,1,0:T(8,128)} %radius_hbm.1, f32[8,16,8,128]{3,2,1,0:T(8,128)} %weight_hbm.1, s32[8,16,8,128]{3,2,1,0:T(8,128)} %column_hbm.1, ...), custom_call_target="tpu_custom_call" | custom-call | tf_op jit(solution)/shard_map/slab_step/pallas_call | solution.py:823
  32.8 0.8 %write_out.1 = (f32[5,16,8,128]{3,2,1,0:T(8,128)}, f32[3,16,8,128]{3,2,1,0:T(8,128)}) custom-call(f32[5,16,8,128]{3,2,1,0:T(8,128)S(1)} %get-tuple-element.4.fields, f32[3,16,8,128]{3,2,1,0:T(8,128)S(1)} %get-tuple-element.5.moments), custom_call_target="tpu_custom_call" | custom-call | tf_op jit(solution)/shard_map/write_out/pallas_call | solution.py:841

commit v4 on v3

--- a/solution.py
+++ b/solution.py
@@ -9,7 +9,7 @@
 
 NS = 4
 FMAX = 8
-CELLS = 8
+CELLS = 4
 SLOT = 8
 EDGE = 3
 CHUNKS = (32, 24, 28, 24, 20)
@@ -570,38 +570,39 @@
         loop(levels, cell, 0, 2)
 
     def deposit(begin, cells):
-        ids = lax.broadcasted_iota(jnp.int32, (cols, cols), 0).astype(jnp.float32).astype(jnp.bfloat16)
-        one = jnp.ones((cols, cols), jnp.bfloat16)
-        none = jnp.zeros((cols, cols), jnp.bfloat16)
-        blank = jnp.zeros((8, cols), jnp.float32)
+        narrow, thin_type = jnp.bfloat16, jnp.float8_e4m3fn
+        ids = lax.broadcasted_iota(jnp.int32, (cols, cols), 0).astype(jnp.float32).astype(narrow)
+        one = jnp.ones((cols, cols), narrow)
+        none = jnp.zeros((cols, cols), narrow)
+        tile = (2 * rows, cols)
+        blank = jnp.zeros(tile, narrow)
+        half = (lax.broadcasted_iota(jnp.int32, tile, 0) // rows).astype(jnp.float32)
+        stairs = [(half + 2.0 * q).astype(narrow) for q in range(FMAX // 2 + 1)]
 
         def cell(n, carry):
             k, j = (begin + n) // rows, (begin + n) % rows
-            by_depth = [None] * (FMAX + 1)
-            for s in range(0, slots, 4):
+            total = None
+            for s in range(0, slots, 2):
                 left, hots = [], []
-                for t in range(4):
-                    v = vals[s + t, k, pl.ds(j, 8, stride=rows), :]
-                    left.append(jnp.concatenate([v, blank] if t % 2 == 0 else [blank, v], axis=1))
-                    c = column[s + t, k, pl.ds(j, 1), :].astype(jnp.float32).astype(jnp.bfloat16)
-                    hots.append(jnp.where(ids == jnp.broadcast_to(c, (cols, cols)), one, none))
-                lhs = jnp.concatenate(left, axis=0).astype(jnp.bfloat16)
-                rhs = jnp.concatenate(
-                    [jnp.concatenate(hots[:2], axis=1), jnp.concatenate(hots[2:], axis=1)], axis=0
+                for t in (s, s + 1):
+                    v = vals[t, k, pl.ds(j, 8, stride=rows), :]
+                    base = jnp.concatenate([v, v], axis=0).astype(narrow)
+                    fall = jnp.full(tile, depth[t, j, 0, k], jnp.int32)
+                    fall = fall.astype(jnp.float32).astype(narrow)
+                    left.append(jnp.concatenate(
+                        [jnp.where(stair == fall, base, blank) for stair in stairs], axis=0
+                    ))
+                    c = column[t, k, pl.ds(j, 1), :].astype(jnp.float32).astype(narrow)
+                    hot = jnp.where(ids == jnp.broadcast_to(c, (cols, cols)), one, none)
+                    hots.append(hot.astype(thin_type))
+                got = lax.dot_general(
+                    jnp.concatenate(left, axis=1), jnp.concatenate(hots, axis=1),
+                    (((1,), (1,)), ((), ())), preferred_element_type=jnp.float32,
                 )
-                got = lax.dot_general(
-                    lhs, rhs, (((1,), (1,)), ((), ())), preferred_element_type=jnp.float32
-                )
-                for t in range(4):
-                    half = t // 2
-                    part = got[8 * t:8 * (t + 1), half * cols:(half + 1) * cols]
-                    fall = depth[s + t, j, 0, k]
-                    for d in range(FMAX + 1):
-                        term = jnp.where(fall == d, part, 0.0)
-                        by_depth[d] = term if by_depth[d] is None else by_depth[d] + term
+                total = got if total is None else total + got
             at = pl.ds(pl.multiple_of(j * 8, 8), 8)
             for d in range(FMAX + 1):
-                fallen[k, d, at, :] = by_depth[d]
+                fallen[k, d, at, :] = total[8 * d:8 * (d + 1)]
             return carry
 
         lax.fori_loop(0, cells, cell, 0, unroll=min(CELLS, cells))

time: 33.7 us -> 31.1 us (0.923)
  Pallas kernels: 32.9 us -> 30.3 us
    pallas_call x1, Pallas kernels: 32.1 us -> 29.5 us  [per_device(): pl.pallas_call(functools.partial(kernel, (tuple(spaces), levels, rows, co...]
where the time goes in v4:
time: 31.1 us; the launch traced here: 31 us
  Pallas kernels  30.3 us (97%)
  between operations  0.64 us (2%)
    pallas_call x1, Pallas kernels, per_device(): pl.pallas_call(functools.partial(kernel, (tuple(spaces), levels, rows, co...  29.5 us
    pallas_call x1, Pallas kernels, per_device(): pl.pallas_call(write_out, out_shape=tuple((jax.ShapeDtypeStruct(r.shape,...  0.8 us

profile of v4, /device:TPU:0, one launch (start us, length us, event | category | flops | bytes accessed | tf_op | source)
XLA Modules:
  0.0 31.0 jit_solution(13964971973890765621)
XLA Ops:
  0.6 29.5 %slab_step.1 = (f32[5,16,8,128]{3,2,1,0:T(8,128)S(1)}, f32[3,16,8,128]{3,2,1,0:T(8,128)S(1)}) custom-call(s32[8,8,1,16]{3,2,1,0:T(1,128)} %bitcast.1, f32[5,16,8,128]{3,2,1,0:T(8,128)} %fields_hbm.1, f32[8,16,8,128]{3,2,1,0:T(8,128)} %radius_hbm.1, f32[8,16,8,128]{3,2,1,0:T(8,128)} %weight_hbm.1, s32[8,16,8,128]{3,2,1,0:T(8,128)} %column_hbm.1, ...), custom_call_target="tpu_custom_call" | custom-call | tf_op jit(solution)/shard_map/slab_step/pallas_call | solution.py:824
  30.2 0.8 %write_out.1 = (f32[5,16,8,128]{3,2,1,0:T(8,128)}, f32[3,16,8,128]{3,2,1,0:T(8,128)}) custom-call(f32[5,16,8,128]{3,2,1,0:T(8,128)S(1)} %get-tuple-element.4.fields, f32[3,16,8,128]{3,2,1,0:T(8,128)S(1)} %get-tuple-element.5.moments), custom_call_target="tpu_custom_call" | custom-call | tf_op jit(solution)/shard_map/write_out/pallas_call | solution.py:842

commit v5 on v4

--- a/solution.py
+++ b/solution.py
@@ -9,10 +9,10 @@
 
 NS = 4
 FMAX = 8
-CELLS = 4
+CELLS = 8
 SLOT = 8
 EDGE = 3
-CHUNKS = (32, 24, 28, 24, 20)
+CHUNKS = (40, 24, 24, 24, 16)
 ONE_SHOT = 32
 KERNEL_BYTES = 40 * 1024 * 1024
 
@@ -38,7 +38,7 @@
     total = 1
     for a in AXES:
         total *= count[a]
-    return (AXES,) if total <= ONE_SHOT else tuple((a,) for a in AXES)
+    return (("gz", "gy", "gx"),) if total <= ONE_SHOT else tuple((a,) for a in AXES)
 
 
 def shifts_of(group, count):
@@ -101,7 +101,7 @@
          (column_hbm, column), (depth_hbm, depth))
     ):
         later_copies.append(pltpu.make_async_copy(src, dst, local_sem.at[5 + n]))
-    for copy in first_copies + later_copies:
+    for copy in first_copies:
         copy.start()
 
     def away(group, shift):
@@ -109,13 +109,15 @@
 
     barrier = pltpu.get_barrier_semaphore()
     peers = 0
-    for step in greeted(groups, count):
+    for step in sorted(greeted(groups, count), key=lambda step: step.get("gz", count["gz"])):
         pl.semaphore_signal(
             barrier, inc=1, device_id=away(tuple(step), tuple(step.values())),
             device_id_type=MESH,
         )
         peers += 1
 
+    for copy in later_copies:
+        copy.start()
     for copy in first_copies:
         copy.wait()
 
@@ -150,7 +152,7 @@
     def max_start(g, value):
         refs["max_send"][g] = value
         copies = []
-        for n, shift in enumerate(shifts_of(groups[g], count)):
+        for n, shift in reversed(list(enumerate(shifts_of(groups[g], count)))):
             copy = pltpu.make_async_remote_copy(
                 src_ref=refs["max_send"].at[g],
                 dst_ref=refs["max_recv"].at[g, n],
@@ -163,8 +165,7 @@
         return copies
 
     def max_end(g, value, copies):
-        for copy in copies:
-            copy.wait()
+        wait(copies)
         for n in range(len(copies)):
             value = jnp.maximum(value, refs["max_recv"][g, n])
         return value
@@ -264,13 +265,7 @@
     def send_full(name, tag):
         sems, e = "f" + tag, FULL[tag]
         at = 0 if name == "P" else 6
-        packed = pack(lambda k: refs[name + tag][k + 3])
         z = z_copies(name, tag, sems, at + 4)
-        if tag == "0" and name == "P":
-            for k in range(levels):
-                wind = lanes_by(refs["U0"][k], SLOT * k + 7)
-                packed = jnp.where((lane // SLOT == k) & (slot_lane == 6), wind, packed)
-        refs["x" + name + "_s"][e] = packed
         if name == "P":
             start(y_copies(name, tag, sems, at + 2))
             if tag == "0":
@@ -278,6 +273,13 @@
                 z_start((z[0], wind_copies()[1]), (z[1],))
             else:
                 z_start((z[0],), (z[1],))
+        packed = pack(lambda k: refs[name + tag][k + 3])
+        if tag == "0" and name == "P":
+            for k in range(levels):
+                wind = lanes_by(refs["U0"][k], SLOT * k + 7)
+                packed = jnp.where((lane // SLOT == k) & (slot_lane == 6), wind, packed)
+        refs["x" + name + "_s"][e] = packed
+        if name == "P":
             start(x_copies("x" + name, e, sems, at))
         else:
             z_start((z[0],), (z[1],))
@@ -318,9 +320,9 @@
     def send_thin(tag):
         sems, e = "t" + tag, THIN[tag]
         z = z_copies("P", tag, sems, 4)
-        refs["tx_s"][e] = pack(lambda k: refs["P" + tag][k + 3])
         start(y_copies("P", tag, sems, 2))
         z_start((z[0],), (z[1],))
+        refs["tx_s"][e] = pack(lambda k: refs["P" + tag][k + 3])
         start(x_copies("tx", e, sems, 0))
 
     def receive_thin(tag, fix=None):
@@ -369,8 +371,8 @@
             refs["dz_s"][e, EDGE + t] = change(tag, levels - EDGE + t)
         refs["d_s"][e] = pack(lambda k: change(tag, k))
         flat, ups, downs = delta_copies(tag)
-        z_start(ups, downs)
-        start(flat)
+        z_start(ups[1:] + ups[:1], downs[1:] + downs[:1])
+        start(flat[4:] + flat[:4])
 
     def receive_delta(tag):
         flat, ups, downs = delta_copies(tag)
@@ -410,6 +412,18 @@
         high = refs["P" + tag][3 + levels] - refs["P0"][3 + levels]
         W[0] = W[0] + push * low
         W[levels] = W[levels] - push * high
+
+        def layers(t, there, wanted, nearest, source, level, at):
+            sides_of = pairs(refs["dxz_lo"][e, t], refs["dxz_hi"][e, t])
+            for n in wanted:
+                part = jnp.where(edge_lane, to_level(sides_of, level + n), 0.0)
+                part = part + jnp.where(edge_row, nearer(refs["dyz"][e, t, n]), 0.0)
+                if n == nearest:
+                    part = part + change(tag, source)
+                P[at + n] = P[at + n] + jnp.where(there, gain * part, 0.0)
+
+        layers(0, has_low, range(EDGE) if full else (EDGE - 1,), EDGE - 1, 0, levels - EDGE, 0)
+        layers(1, has_high, range(EDGE) if full else (0,), 0, levels - 1, 0, 3 + levels)
         for k in range(levels):
             own = change(tag, k)
             dx = jnp.where(edge_lane, to_level(face, k), 0.0)
@@ -435,23 +449,6 @@
             else:
                 refs["HYT" + p_tag][k] = refs["HYT" + p_tag][k] + gain * nearer(beside)
 
-        def layers(t, wanted, nearest, source, level, at):
-            sides_of = pairs(refs["dxz_lo"][e, t], refs["dxz_hi"][e, t])
-            for n in wanted:
-                part = jnp.where(edge_lane, to_level(sides_of, level + n), 0.0)
-                part = part + jnp.where(edge_row, nearer(refs["dyz"][e, t, n]), 0.0)
-                if n == nearest:
-                    part = part + change(tag, source)
-                P[at + n] = P[at + n] + gain * part
-
-        @pl.when(has_low)
-        def _():
-            layers(0, range(EDGE) if full else (EDGE - 1,), EDGE - 1, 0, levels - EDGE, 0)
-
-        @pl.when(has_high)
-        def _():
-            layers(1, range(EDGE) if full else (0,), 0, levels - 1, 0, 3 + levels)
-
     def sides(q, halo, by, index, extent):
         low = [by(jnp.where(index >= extent - n, halo, q), n) for n in (3, 2, 1)]
         high = [by(jnp.where(index < n, halo, q), -n) for n in (1, 2, 3)]
@@ -518,12 +515,15 @@
             w = vertical(k + 1)
             if k == levels - 1:
                 w = w * lid_high
+            hu, hv = HXU[k], HYV[k]
             u_new = u - push * (jnp.where(lane == cols - 1, hx, lanes_by(p, -1)) - p)
             v_new = v - push * (jnp.where(row == rows - 1, hy, rows_by(p, -1)) - p)
-            u_halo = HXU[k] - push * (p - hx)
-            v_halo = HYV[k] - push * (p - hy)
-            u_low = jnp.where(lane == 0, u_halo, lanes_by(u_new, 1))
-            v_low = jnp.where(row == 0, v_halo, rows_by(v_new, 1))
+            u_halo = u_low = jnp.where(lane == 0, hu, lanes_by(u, 1)) - push * (
+                p - jnp.where(lane == 0, hx, lanes_by(p, 1))
+            )
+            v_halo = v_low = jnp.where(row == 0, hv, rows_by(v, 1)) - push * (
+                p - jnp.where(row == 0, hy, rows_by(p, 1))
+            )
             div = (u_new - u_low) + (v_new - v_low) + (w - w_low)
             p_new = p + sub_step * (refs["rate_p"][k] - sound_speed * div)
             w_low = w
@@ -746,10 +746,10 @@
 
 
 def write_out(fields, moments, out_fields, out_moments, sem):
-    copies = [
-        pltpu.make_async_copy(fields, out_fields, sem.at[0]),
-        pltpu.make_async_copy(moments, out_moments, sem.at[1]),
-    ]
+    copies = []
+    for source, out in ((fields, out_fields), (moments, out_moments)):
+        for n in range(source.shape[0]):
+            copies.append(pltpu.make_async_copy(source.at[n], out.at[n], sem.at[len(copies)]))
     for copy in copies:
         copy.start()
     for copy in copies:
@@ -844,7 +844,7 @@
         out_shape=tuple(jax.ShapeDtypeStruct(r.shape, f32) for r in results),
         in_specs=[vmem] * 2,
         out_specs=(anywhere,) * 2,
-        scratch_shapes=[pltpu.SemaphoreType.DMA((2,))],
+        scratch_shapes=[pltpu.SemaphoreType.DMA((sum(r.shape[0] for r in results),))],
         compiler_params=pltpu.CompilerParams(vmem_limit_bytes=1024 * 1024),
         name="write_out",
     )(*results)

time: 31.1 us -> 30.1 us (0.968)
  Pallas kernels: 30.3 us -> 29.3 us
    pallas_call x1, Pallas kernels: 29.5 us -> 28.5 us  [per_device(): pl.pallas_call(functools.partial(kernel, (tuple(spaces), levels, rows, co...]
where the time goes in v5:
time: 30.1 us; the launch traced here: 30 us
  Pallas kernels  29.3 us (97%)
  between operations  0.64 us (2%)
    pallas_call x1, Pallas kernels, per_device(): pl.pallas_call(functools.partial(kernel, (tuple(spaces), levels, rows, co...  28.5 us
    pallas_call x1, Pallas kernels, per_device(): pl.pallas_call(write_out, out_shape=tuple((jax.ShapeDtypeStruct(r.shape,...  0.85 us

profile of v5, /device:TPU:0, one launch (start us, length us, event | category | flops | bytes accessed | tf_op | source)
XLA Modules:
  0.0 30.0 jit_solution(9199704666741982885)
XLA Ops:
  0.6 28.5 %slab_step.1 = (f32[5,16,8,128]{3,2,1,0:T(8,128)S(1)}, f32[3,16,8,128]{3,2,1,0:T(8,128)S(1)}) custom-call(s32[8,8,1,16]{3,2,1,0:T(1,128)} %bitcast.1, f32[5,16,8,128]{3,2,1,0:T(8,128)} %fields_hbm.1, f32[8,16,8,128]{3,2,1,0:T(8,128)} %radius_hbm.1, f32[8,16,8,128]{3,2,1,0:T(8,128)} %weight_hbm.1, s32[8,16,8,128]{3,2,1,0:T(8,128)} %column_hbm.1, ...), custom_call_target="tpu_custom_call" | custom-call | tf_op jit(solution)/shard_map/slab_step/pallas_call | solution.py:824
  29.1 0.9 %write_out.1 = (f32[5,16,8,128]{3,2,1,0:T(8,128)}, f32[3,16,8,128]{3,2,1,0:T(8,128)}) custom-call(f32[5,16,8,128]{3,2,1,0:T(8,128)S(1)} %get-tuple-element.4.fields, f32[3,16,8,128]{3,2,1,0:T(8,128)S(1)} %get-tuple-element.5.moments), custom_call_target="tpu_custom_call" | custom-call | tf_op jit(solution)/shard_map/write_out/pallas_call | solution.py:842

commit v6 on v5

--- a/solution.py
+++ b/solution.py
@@ -146,7 +146,8 @@
         return jnp.maximum(top, speed)
 
     top = loop(levels, fastest, zero)
-    top = jnp.max(top, axis=0, keepdims=True)
+    top = jnp.max(top, axis=(0, 1), keepdims=True)
+    top = jnp.broadcast_to(top, (1, cols))
     pl.semaphore_wait(barrier, peers)
 
     def max_start(g, value):
@@ -289,6 +290,10 @@
     def receive_x(name, tag, fix=None):
         sems, e = "f" + tag, FULL[tag]
         wait(x_copies("x" + name, e, sems, 0 if name == "P" else 6))
+        if fix is not None:
+            receive_z(name, tag)
+            receive_y(name, tag)
+            fix = fix()
         low, high = refs["x" + name + "_lo"][e], refs["x" + name + "_hi"][e]
         both = jnp.where(slot_lane < EDGE, low, high)
         if fix is not None:
@@ -331,12 +336,16 @@
         wait(x_copies("tx", e, sems, 0))
         low, high = refs["tx_lo"][e], refs["tx_hi"][e]
         if fix is not None:
+            z_wait((z[0],), (z[1],))
+            wait(y_copies("P", tag, sems, 2))
+            fix = fix()
             low, high = low + fix, high + fix
         both = pairs(low, high)
         for k in range(levels):
             refs["HXT" + tag][k] = to_level(both, k)
-        z_wait((z[0],), (z[1],))
-        wait(y_copies("P", tag, sems, 2))
+        if fix is None:
+            z_wait((z[0],), (z[1],))
+            wait(y_copies("P", tag, sems, 2))
 
     def change(tag, k):
         return refs["P" + tag][k + 3] - refs["P0"][k + 3]
@@ -524,8 +533,9 @@
             v_halo = v_low = jnp.where(row == 0, hv, rows_by(v, 1)) - push * (
                 p - jnp.where(row == 0, hy, rows_by(p, 1))
             )
-            div = (u_new - u_low) + (v_new - v_low) + (w - w_low)
-            p_new = p + sub_step * (refs["rate_p"][k] - sound_speed * div)
+            if last:
+                div = (u_new - u_low) + (v_new - v_low) + (w - w_low)
+                p_new = p + sub_step * (refs["rate_p"][k] - sound_speed * div)
             w_low = w
             if last:
                 for n, part in enumerate((p_new, u_new, v_new, w)):
@@ -536,7 +546,62 @@
                 refs["W" + dw][k + 1] = w
                 refs["HXU" + dw][k] = u_halo
                 refs["HYV" + dw][k] = v_halo
-                refs["P" + dp][k + 3] = p_new
+
+    def spread_of(p, hx, hy):
+        east = jnp.where(lane == cols - 1, hx, lanes_by(p, -1))
+        west = jnp.where(lane == 0, hx, lanes_by(p, 1))
+        north = jnp.where(row == rows - 1, hy, rows_by(p, -1))
+        south = jnp.where(row == 0, hy, rows_by(p, 1))
+        return ((east - p) + (west - p)) + ((north - p) + (south - p))
+
+    def lids():
+        return jnp.where(has_low, 1.0, 0.0), jnp.where(has_high, 1.0, 0.0)
+
+    def first_parts():
+        P, U, V, W = (refs[n + "0"] for n in "PUVW")
+        lid_low, lid_high = lids()
+        low = (P[3] - P[2]) * lid_low
+        for k in range(levels):
+            p, u, v = P[k + 3], U[k], V[k]
+            high = P[k + 4] - p
+            if k == levels - 1:
+                high = high * lid_high
+            u_low = jnp.where(lane == 0, refs["HXU0"][k], lanes_by(u, 1))
+            v_low = jnp.where(row == 0, refs["HYV0"][k], rows_by(v, 1))
+            refs["div"][k] = (u - u_low) + (v - v_low) + (W[k + 1] - W[k])
+            refs["bend"][k] = spread_of(p, refs["HXT0"][k], refs["HYT0"][k]) + (high - low)
+            low = high
+
+    def press_first(dp, sub_step):
+        push = sub_step * sound_speed
+        for k in range(levels):
+            rate = refs["rate_p"][k] - sound_speed * refs["div"][k]
+            lift = sound_speed * refs["bend"][k] - (refs["lift"][k + 1] - refs["lift"][k])
+            refs["P" + dp][k + 3] = refs["P0"][k + 3] + sub_step * (rate + push * lift)
+
+    def press(sp, hp, pp, dp, sub_step):
+        SP, HP, PP, DP = (refs["P" + t] for t in (sp, hp, pp, dp))
+        push = sub_step * sound_speed
+        lid_low, lid_high = lids()
+
+        def rise(k):
+            above = (HP if k == levels else SP)[k + 3]
+            below = (HP if k == 0 else SP)[k + 2]
+            return refs["lift"][k] - sound_speed * (above - below)
+
+        low = rise(0) * lid_low
+        for k in range(levels):
+            p = SP[k + 3]
+            high = rise(k + 1)
+            if k == levels - 1:
+                high = high * lid_high
+            spread = spread_of(p, refs["HXT" + hp][k], refs["HYT" + hp][k])
+            gain = (push * sub_step) * (sound_speed * spread - (high - low))
+            DP[k + 3] = (p + (p - PP[k + 3])) + gain
+            low = high
+
+    def winds(sp, hp, sw, dw, sub_step):
+        substep(sp, hp, sw, "", dw, sub_step)
 
     def tracer(tag, scale):
         for k in range(levels):
@@ -667,15 +732,16 @@
     receive_z("P", "0")
     advect("P", "0", "rate_p")
     first_edges()
+    first_parts()
     receive_z("C", "0")
     lift_of("0")
     top = max_end(len(groups) - 1, top, copies)
-    time_step = courant_goal / (1.0 + jnp.max(top, axis=(0, 1), keepdims=True))
-    time_step = jnp.broadcast_to(time_step, shape)
+    time_step = jnp.broadcast_to(courant_goal / (1.0 + top), shape)
 
     third = time_step * (1.0 / 3.0)
-    substep("0", "0", "0", "1", "1", third)
+    press_first("1", third)
     send_full("P", "1")
+    winds("0", "0", "0", "1", third)
     tracer_section("0")
     tracer("1", third)
     send_full("C", "1")
@@ -688,31 +754,33 @@
     lift_of("1")
     half = time_step * 0.5
     part = half / (NS // 2)
-    substep("0", "0", "0", "a", "a", part)
+    press_first("a", part)
     send_delta("a")
-    substep("a", "0", "a", "2", "2", part)
+    press("a", "0", "0", "2", part)
     send_full("P", "2")
+    winds("0", "0", "0", "a", part)
+    winds("a", "0", "a", "2", part)
     tracer_section("1")
     tracer("2", half)
     send_full("C", "2")
     chunk(2)
     fall_send(0)
 
+    push = part * sound_speed
     receive_delta("a")
-    push = part * sound_speed
-    receive_x("P", "2", push * push * packed_fix("a"))
-    receive_z("P", "2")
-    receive_y("P", "2")
+    receive_x("P", "2", lambda: push * push * packed_fix("a"))
     mend("a", "2", "2", push)
     advect_xz("P", "2", "rate_p")
     advect_y("P", "2", "rate_p")
     receive_z("C", "2")
     lift_of("2")
     part = time_step / NS
-    substep("0", "0", "0", "b", "b", part)
+    press_first("b", part)
     send_delta("b")
-    substep("b", "0", "b", "c", "c", part)
+    press("b", "0", "0", "c", part)
     send_thin("c")
+    winds("0", "0", "0", "b", part)
+    winds("b", "0", "b", "c", part)
     tracer_section("2")
     tracer(None, time_step)
     fall_send(1)
@@ -721,10 +789,11 @@
 
     receive_delta("b")
     push = part * sound_speed
-    receive_thin("c", push * push * packed_fix("b"))
+    receive_thin("c", lambda: push * push * packed_fix("b"))
     mend("b", "c", "c", push)
-    substep("c", "c", "c", "d", "c", part)
+    press("c", "c", "b", "d", part)
     send_thin("d")
+    winds("c", "c", "c", "c", part)
     chunk(4)
     for m in range(3):
         fall_home(m)
@@ -793,6 +862,8 @@
     add("rate_p", levels, *cell)
     add("lift", levels + 1, *cell)
     add("swell", 2, levels, *cell)
+    add("div", levels, *cell)
+    add("bend", levels, *cell)
     add("max_send", len(groups), 1, cols)
     add("max_recv", len(groups), widest, 1, cols)
     for end in ("_s", "_lo", "_hi"):

time: 30.1 us -> 29.6 us (0.983)
  Pallas kernels: 29.3 us -> 28.8 us
    pallas_call x1, Pallas kernels: 28.5 us -> 28 us  [per_device(): pl.pallas_call(functools.partial(kernel, (tuple(spaces), levels, rows, co...]
where the time goes in v6:
time: 29.6 us; the launch traced here: 29.5 us
  Pallas kernels  28.8 us (97%)
  between operations  0.64 us (2%)
    pallas_call x1, Pallas kernels, per_device(): pl.pallas_call(functools.partial(kernel, (tuple(spaces), levels, rows, co...  28 us
    pallas_call x1, Pallas kernels, per_device(): pl.pallas_call(write_out, out_shape=tuple((jax.ShapeDtypeStruct(r.shape,...  0.85 us

profile of v6, /device:TPU:0, one launch (start us, length us, event | category | flops | bytes accessed | tf_op | source)
XLA Modules:
  0.0 29.5 jit_solution(18383903403570497325)
XLA Ops:
  0.6 28.0 %slab_step.1 = (f32[5,16,8,128]{3,2,1,0:T(8,128)S(1)}, f32[3,16,8,128]{3,2,1,0:T(8,128)S(1)}) custom-call(s32[8,8,1,16]{3,2,1,0:T(1,128)} %bitcast.1, f32[5,16,8,128]{3,2,1,0:T(8,128)} %fields_hbm.1, f32[8,16,8,128]{3,2,1,0:T(8,128)} %radius_hbm.1, f32[8,16,8,128]{3,2,1,0:T(8,128)} %weight_hbm.1, s32[8,16,8,128]{3,2,1,0:T(8,128)} %column_hbm.1, ...), custom_call_target="tpu_custom_call" | custom-call | tf_op jit(solution)/shard_map/slab_step/pallas_call | solution.py:895
  28.6 0.9 %write_out.1 = (f32[5,16,8,128]{3,2,1,0:T(8,128)}, f32[3,16,8,128]{3,2,1,0:T(8,128)}) custom-call(f32[5,16,8,128]{3,2,1,0:T(8,128)S(1)} %get-tuple-element.4.fields, f32[3,16,8,128]{3,2,1,0:T(8,128)S(1)} %get-tuple-element.5.moments), custom_call_target="tpu_custom_call" | custom-call | tf_op jit(solution)/shard_map/write_out/pallas_call | solution.py:913

commit v7 on v6

--- a/solution.py
+++ b/solution.py
@@ -26,6 +26,10 @@
 FULL = {"0": 0, "1": 1, "2": 2}
 THIN = {"c": 0, "d": 1}
 DELTA = {"a": 0, "b": 1}
+
+
+class Named(dict):
+    __getattr__ = dict.__getitem__
 
 
 def flux(wind, a, b, c, d, e, f):
@@ -64,11 +68,11 @@
     out_fields, moments, *scratch
 ):
     names, levels, rows, cols, slots = sizes
-    refs = dict(zip(names, scratch))
+    refs = Named(zip(names, scratch))
     radius, weight, column, counts = (refs[n] for n in ("radius", "weight", "column", "counts"))
-    depth = refs["depth"]
-    vals, fallen = refs["vals"], refs["fallen"]
-    local_sem = refs["local_sem"]
+    depth = refs.depth
+    vals, fallen = refs.vals, refs.fallen
+    local_sem = refs.local_sem
     shape = (rows, cols)
     lane = lax.broadcasted_iota(jnp.int32, shape, 1)
     row = lax.broadcasted_iota(jnp.int32, shape, 0)
@@ -91,8 +95,8 @@
 
     first_copies = []
     for n, dst in enumerate(
-        (refs["C0"].at[pl.ds(3, levels)], refs["P0"].at[pl.ds(3, levels)],
-         refs["U0"], refs["V0"], refs["W0"].at[pl.ds(1, levels)])
+        (refs.C0.at[pl.ds(3, levels)], refs.P0.at[pl.ds(3, levels)],
+         refs.U0, refs.V0, refs.W0.at[pl.ds(1, levels)])
     ):
         first_copies.append(pltpu.make_async_copy(fields_hbm.at[n], dst, local_sem.at[n]))
     later_copies = []
@@ -123,7 +127,7 @@
 
     @pl.when(jnp.logical_not(has_high))
     def _():
-        refs["W0"][levels] = zero
+        refs.W0[levels] = zero
         for tag in ("0", "1", "2"):
             for t in range(EDGE):
                 refs["C" + tag][3 + levels + t] = zero
@@ -133,7 +137,7 @@
 
     @pl.when(jnp.logical_not(has_low))
     def _():
-        refs["W0"][0] = zero
+        refs.W0[0] = zero
         for tag in ("0", "1", "2"):
             for t in range(EDGE):
                 refs["C" + tag][t] = zero
@@ -142,7 +146,7 @@
                 refs["P" + tag][t] = zero
 
     def fastest(k, top):
-        speed = jnp.abs(refs["U0"][k]) + jnp.abs(refs["V0"][k]) + jnp.abs(refs["W0"][k + 1])
+        speed = jnp.abs(refs.U0[k]) + jnp.abs(refs.V0[k]) + jnp.abs(refs.W0[k + 1])
         return jnp.maximum(top, speed)
 
     top = loop(levels, fastest, zero)
@@ -151,14 +155,14 @@
     pl.semaphore_wait(barrier, peers)
 
     def max_start(g, value):
-        refs["max_send"][g] = value
+        refs.max_send[g] = value
         copies = []
         for n, shift in reversed(list(enumerate(shifts_of(groups[g], count)))):
             copy = pltpu.make_async_remote_copy(
-                src_ref=refs["max_send"].at[g],
-                dst_ref=refs["max_recv"].at[g, n],
-                send_sem=refs["max_ss"].at[g, n],
-                recv_sem=refs["max_rs"].at[g, n],
+                src_ref=refs.max_send.at[g],
+                dst_ref=refs.max_recv.at[g, n],
+                send_sem=refs.max_ss.at[g, n],
+                recv_sem=refs.max_rs.at[g, n],
                 device_id=away(groups[g], shift), device_id_type=MESH,
             )
             copy.start()
@@ -168,7 +172,7 @@
     def max_end(g, value, copies):
         wait(copies)
         for n in range(len(copies)):
-            value = jnp.maximum(value, refs["max_recv"][g, n])
+            value = jnp.maximum(value, refs.max_recv[g, n])
         return value
 
     def neighbour(*steps):
@@ -245,10 +249,10 @@
                 copy.wait_recv()
 
     def wind_copies():
-        own = refs["V0"].at[:, pl.ds(rows - 1, 1), :]
+        own = refs.V0.at[:, pl.ds(rows - 1, 1), :]
         return (
-            remote(own, refs["HYV0"].at[:, pl.ds(0, 1), :], "f0", 12, "gy", 1),
-            remote(refs["W0"].at[levels], refs["W0"].at[0], "f0", 13, "gz", 1),
+            remote(own, refs.HYV0.at[:, pl.ds(0, 1), :], "f0", 12, "gy", 1),
+            remote(refs.W0.at[levels], refs.W0.at[0], "f0", 13, "gz", 1),
         )
 
     def pack(value, packed=None):
@@ -277,7 +281,7 @@
         packed = pack(lambda k: refs[name + tag][k + 3])
         if tag == "0" and name == "P":
             for k in range(levels):
-                wind = lanes_by(refs["U0"][k], SLOT * k + 7)
+                wind = lanes_by(refs.U0[k], SLOT * k + 7)
                 packed = jnp.where((lane // SLOT == k) & (slot_lane == 6), wind, packed)
         refs["x" + name + "_s"][e] = packed
         if name == "P":
@@ -302,7 +306,7 @@
             refs["HX" + name + tag][k] = to_level(both, k)
         if tag == "0" and name == "P":
             for k in range(levels):
-                refs["HXU0"][k] = lanes_by(low, -(SLOT * k + 6))
+                refs.HXU0[k] = lanes_by(low, -(SLOT * k + 6))
 
     def receive_z(name, tag):
         z = z_copies(name, tag, "f" + tag, 4 if name == "P" else 10)
@@ -318,23 +322,23 @@
 
     def first_edges():
         for k in range(levels):
-            x, y = refs["HXP0"][k], refs["HYP0"][k]
-            refs["HXT0"][k] = jnp.where(lane == 0, lanes_by(x, 1), lanes_by(x, -1))
-            refs["HYT0"][k] = jnp.where(row == 0, rows_by(y, 1), rows_by(y, -1))
+            x, y = refs.HXP0[k], refs.HYP0[k]
+            refs.HXT0[k] = jnp.where(lane == 0, lanes_by(x, 1), lanes_by(x, -1))
+            refs.HYT0[k] = jnp.where(row == 0, rows_by(y, 1), rows_by(y, -1))
 
     def send_thin(tag):
         sems, e = "t" + tag, THIN[tag]
         z = z_copies("P", tag, sems, 4)
         start(y_copies("P", tag, sems, 2))
         z_start((z[0],), (z[1],))
-        refs["tx_s"][e] = pack(lambda k: refs["P" + tag][k + 3])
+        refs.tx_s[e] = pack(lambda k: refs["P" + tag][k + 3])
         start(x_copies("tx", e, sems, 0))
 
     def receive_thin(tag, fix=None):
         sems, e = "t" + tag, THIN[tag]
         z = z_copies("P", tag, sems, 4)
         wait(x_copies("tx", e, sems, 0))
-        low, high = refs["tx_lo"][e], refs["tx_hi"][e]
+        low, high = refs.tx_lo[e], refs.tx_hi[e]
         if fix is not None:
             z_wait((z[0],), (z[1],))
             wait(y_copies("P", tag, sems, 2))
@@ -348,14 +352,14 @@
             wait(y_copies("P", tag, sems, 2))
 
     def change(tag, k):
-        return refs["P" + tag][k + 3] - refs["P0"][k + 3]
+        return refs["P" + tag][k + 3] - refs.P0[k + 3]
 
     top_rows, low_rows = pl.ds(rows - EDGE, EDGE), pl.ds(0, EDGE)
     top_levels, low_levels = pl.ds(EDGE, EDGE), pl.ds(0, EDGE)
 
     def delta_copies(tag):
         e, sems = DELTA[tag], "d" + tag
-        s, dz = refs["d_s"].at[e], refs["dz_s"].at[e]
+        s, dz = refs.d_s.at[e], refs.dz_s.at[e]
         flat = list(x_copies("d", e, sems, 0)) + list(y_copies("P", tag, sems, 2))
         for n, (end, sx) in enumerate((("lo", 1), ("hi", -1))):
             dst = refs["dxy_" + end].at[e]
@@ -369,16 +373,16 @@
                 found.append(remote(s, refs["dxz_" + end].at[e, t], sems, 10 + 2 * t + n,
                                     "gx", sx, "gz", sz))
             for n, (part_y, sy) in enumerate(((top_rows, 1), (low_rows, -1))):
-                found.append(remote(dz.at[part, part_y, :], refs["dyz"].at[e, t, :, part_y, :],
+                found.append(remote(dz.at[part, part_y, :], refs.dyz.at[e, t, :, part_y, :],
                                     sems, 14 + 2 * t + n, "gy", sy, "gz", sz))
         return flat, ups, downs
 
     def send_delta(tag):
         e = DELTA[tag]
         for t in range(EDGE):
-            refs["dz_s"][e, t] = change(tag, t)
-            refs["dz_s"][e, EDGE + t] = change(tag, levels - EDGE + t)
-        refs["d_s"][e] = pack(lambda k: change(tag, k))
+            refs.dz_s[e, t] = change(tag, t)
+            refs.dz_s[e, EDGE + t] = change(tag, levels - EDGE + t)
+        refs.d_s[e] = pack(lambda k: change(tag, k))
         flat, ups, downs = delta_copies(tag)
         z_start(ups[1:] + ups[:1], downs[1:] + downs[:1])
         start(flat[4:] + flat[:4])
@@ -396,10 +400,10 @@
 
     def packed_fix(tag):
         e = DELTA[tag]
-        d = refs["d_s"][e]
-        across = jnp.where(slot_lane < EDGE, refs["dxy_lo"][e], refs["dxy_hi"][e])
-        below = jnp.where(slot_lane < EDGE, refs["dxz_lo"][e, 0], refs["dxz_hi"][e, 0])
-        above = jnp.where(slot_lane < EDGE, refs["dxz_lo"][e, 1], refs["dxz_hi"][e, 1])
+        d = refs.d_s[e]
+        across = jnp.where(slot_lane < EDGE, refs.dxy_lo[e], refs.dxy_hi[e])
+        below = jnp.where(slot_lane < EDGE, refs.dxz_lo[e, 0], refs.dxz_hi[e, 0])
+        above = jnp.where(slot_lane < EDGE, refs.dxz_lo[e, 1], refs.dxz_hi[e, 1])
         last = SLOT * (levels - 1)
         fix = jnp.where(
             slot_lane == EDGE - 1, lanes_by(d, -1),
@@ -415,18 +419,18 @@
             "P" + p_tag, "U" + w_tag, "V" + w_tag, "W" + w_tag, "HXU" + w_tag, "HYV" + w_tag,
         ))
         full = p_tag in FULL
-        face = pairs(refs["d_lo"][e], refs["d_hi"][e])
-        corner = pairs(refs["dxy_lo"][e], refs["dxy_hi"][e])
-        low = refs["P" + tag][2] - refs["P0"][2]
-        high = refs["P" + tag][3 + levels] - refs["P0"][3 + levels]
+        face = pairs(refs.d_lo[e], refs.d_hi[e])
+        corner = pairs(refs.dxy_lo[e], refs.dxy_hi[e])
+        low = refs["P" + tag][2] - refs.P0[2]
+        high = refs["P" + tag][3 + levels] - refs.P0[3 + levels]
         W[0] = W[0] + push * low
         W[levels] = W[levels] - push * high
 
         def layers(t, there, wanted, nearest, source, level, at):
-            sides_of = pairs(refs["dxz_lo"][e, t], refs["dxz_hi"][e, t])
+            sides_of = pairs(refs.dxz_lo[e, t], refs.dxz_hi[e, t])
             for n in wanted:
                 part = jnp.where(edge_lane, to_level(sides_of, level + n), 0.0)
-                part = part + jnp.where(edge_row, nearer(refs["dyz"][e, t, n]), 0.0)
+                part = part + jnp.where(edge_row, nearer(refs.dyz[e, t, n]), 0.0)
                 if n == nearest:
                     part = part + change(tag, source)
                 P[at + n] = P[at + n] + jnp.where(there, gain * part, 0.0)
@@ -436,7 +440,7 @@
         for k in range(levels):
             own = change(tag, k)
             dx = jnp.where(edge_lane, to_level(face, k), 0.0)
-            dy = jnp.where(edge_row, refs["HYT" + tag][k] - refs["HYT0"][k], 0.0)
+            dy = jnp.where(edge_row, refs["HYT" + tag][k] - refs.HYT0[k], 0.0)
             total = dx + dy
             if k == 0:
                 total = total + low
@@ -450,9 +454,9 @@
             beside = jnp.where(edge_row, jnp.where(row == 0, rows_by(own, 1), rows_by(own, -1)), 0.0)
             beside = beside + jnp.where(edge_lane, to_level(corner, k), 0.0)
             if k == 0:
-                beside = beside + jnp.where(has_low, refs["dyz"][e, 0, EDGE - 1], 0.0)
+                beside = beside + jnp.where(has_low, refs.dyz[e, 0, EDGE - 1], 0.0)
             if k == levels - 1:
-                beside = beside + jnp.where(has_high, refs["dyz"][e, 1, 0], 0.0)
+                beside = beside + jnp.where(has_high, refs.dyz[e, 1, 0], 0.0)
             if full:
                 refs["HYP" + p_tag][k] = refs["HYP" + p_tag][k] + gain * beside
             else:
@@ -500,7 +504,7 @@
                 lift = lift * lid_low
             if k == levels:
                 lift = lift * lid_high
-            refs["lift"][k] = lift
+            refs.lift[k] = lift
 
     def substep(sp, hp, sw, dp, dw, sub_step):
         SP, HP, HXT, HYT = refs["P" + sp], refs["P" + hp], refs["HXT" + hp], refs["HYT" + hp]
@@ -513,7 +517,7 @@
         def vertical(k):
             above = (HP if k == levels else SP)[k + 3]
             below = (HP if k == 0 else SP)[k + 2]
-            return SW[k] + sub_step * (refs["lift"][k] - sound_speed * (above - below))
+            return SW[k] + sub_step * (refs.lift[k] - sound_speed * (above - below))
 
         w_low = vertical(0) * lid_low
         if not last:
@@ -535,7 +539,7 @@
             )
             if last:
                 div = (u_new - u_low) + (v_new - v_low) + (w - w_low)
-                p_new = p + sub_step * (refs["rate_p"][k] - sound_speed * div)
+                p_new = p + sub_step * (refs.rate_p[k] - sound_speed * div)
             w_low = w
             if last:
                 for n, part in enumerate((p_new, u_new, v_new, w)):
@@ -566,18 +570,18 @@
             high = P[k + 4] - p
             if k == levels - 1:
                 high = high * lid_high
-            u_low = jnp.where(lane == 0, refs["HXU0"][k], lanes_by(u, 1))
-            v_low = jnp.where(row == 0, refs["HYV0"][k], rows_by(v, 1))
-            refs["div"][k] = (u - u_low) + (v - v_low) + (W[k + 1] - W[k])
-            refs["bend"][k] = spread_of(p, refs["HXT0"][k], refs["HYT0"][k]) + (high - low)
+            u_low = jnp.where(lane == 0, refs.HXU0[k], lanes_by(u, 1))
+            v_low = jnp.where(row == 0, refs.HYV0[k], rows_by(v, 1))
+            refs.div[k] = (u - u_low) + (v - v_low) + (W[k + 1] - W[k])
+            refs.bend[k] = spread_of(p, refs.HXT0[k], refs.HYT0[k]) + (high - low)
             low = high
 
     def press_first(dp, sub_step):
         push = sub_step * sound_speed
         for k in range(levels):
-            rate = refs["rate_p"][k] - sound_speed * refs["div"][k]
-            lift = sound_speed * refs["bend"][k] - (refs["lift"][k + 1] - refs["lift"][k])
-            refs["P" + dp][k + 3] = refs["P0"][k + 3] + sub_step * (rate + push * lift)
+            rate = refs.rate_p[k] - sound_speed * refs.div[k]
+            lift = sound_speed * refs.bend[k] - (refs.lift[k + 1] - refs.lift[k])
+            refs["P" + dp][k + 3] = refs.P0[k + 3] + sub_step * (rate + push * lift)
 
     def press(sp, hp, pp, dp, sub_step):
         SP, HP, PP, DP = (refs["P" + t] for t in (sp, hp, pp, dp))
@@ -587,7 +591,7 @@
         def rise(k):
             above = (HP if k == levels else SP)[k + 3]
             below = (HP if k == 0 else SP)[k + 2]
-            return refs["lift"][k] - sound_speed * (above - below)
+            return refs.lift[k] - sound_speed * (above - below)
 
         low = rise(0) * lid_low
         for k in range(levels):
@@ -605,12 +609,12 @@
 
     def tracer(tag, scale):
         for k in range(levels):
-            value = refs["C0"][k + 3] + scale * refs["rate_c"][k]
+            value = refs.C0[k + 3] + scale * refs.rate_c[k]
             if tag is None:
                 out_fields[0, k] = value
                 swell = jnp.exp(growth * value)
-                refs["swell"][0, k] = swell
-                refs["swell"][1, k] = swell * jnp.sqrt(swell)
+                refs.swell[0, k] = swell
+                refs.swell[1, k] = swell * jnp.sqrt(swell)
             else:
                 refs["C" + tag][k + 3] = value
 
@@ -683,16 +687,16 @@
                 + fallen[k, d, pl.ds(m + 3, rows, stride=8), :]
             )
             if m:
-                part = part * refs["swell"][m - 1, k]
+                part = part * refs.swell[m - 1, k]
             total = part if total is None else total + part
         return total
 
     def fall_copy(m):
-        return remote(refs["fall_s"].at[m], refs["fall_r"].at[m], "fall", m, "gz", -1)
+        return remote(refs.fall_s.at[m], refs.fall_r.at[m], "fall", m, "gz", -1)
 
     def fall_send(m):
         for l in range(FMAX):
-            refs["fall_s"][m, l] = landed(m, l - FMAX)
+            refs.fall_s[m, l] = landed(m, l - FMAX)
 
         @pl.when(has_low)
         def _():
@@ -811,7 +815,7 @@
             fall_copy(m).wait_recv()
             for l in range(FMAX):
                 at = levels - FMAX + l
-                moments[m, at] = moments[m, at] + refs["fall_r"][m, l]
+                moments[m, at] = moments[m, at] + refs.fall_r[m, l]
 
 
 def write_out(fields, moments, out_fields, out_moments, sem):

time: 29.6 us -> 29.6 us (level)
  no operation moved by 1% of the time
where the time goes in v7:
time: 29.6 us; the launch traced here: 29.5 us
  Pallas kernels  28.8 us (97%)
  between operations  0.64 us (2%)
    pallas_call x1, Pallas kernels, per_device(): pl.pallas_call(functools.partial(kernel, (tuple(spaces), levels, rows, co...  28 us
    pallas_call x1, Pallas kernels, per_device(): pl.pallas_call(write_out, out_shape=tuple((jax.ShapeDtypeStruct(r.shape,...  0.85 us

profile of v7, /device:TPU:0, one launch (start us, length us, event | category | flops | bytes accessed | tf_op | source)
XLA Modules:
  0.0 29.5 jit_solution(18383903403570497325)
XLA Ops:
  0.6 28.0 %slab_step.1 = (f32[5,16,8,128]{3,2,1,0:T(8,128)S(1)}, f32[3,16,8,128]{3,2,1,0:T(8,128)S(1)}) custom-call(s32[8,8,1,16]{3,2,1,0:T(1,128)} %bitcast.1, f32[5,16,8,128]{3,2,1,0:T(8,128)} %fields_hbm.1, f32[8,16,8,128]{3,2,1,0:T(8,128)} %radius_hbm.1, f32[8,16,8,128]{3,2,1,0:T(8,128)} %weight_hbm.1, s32[8,16,8,128]{3,2,1,0:T(8,128)} %column_hbm.1, ...), custom_call_target="tpu_custom_call" | custom-call | tf_op jit(solution)/shard_map/slab_step/pallas_call | solution.py:899
  28.6 0.9 %write_out.1 = (f32[5,16,8,128]{3,2,1,0:T(8,128)}, f32[3,16,8,128]{3,2,1,0:T(8,128)}) custom-call(f32[5,16,8,128]{3,2,1,0:T(8,128)S(1)} %get-tuple-element.4.fields, f32[3,16,8,128]{3,2,1,0:T(8,128)S(1)} %get-tuple-element.5.moments), custom_call_target="tpu_custom_call" | custom-call | tf_op jit(solution)/shard_map/write_out/pallas_call | solution.py:917
